TPU v7x, 32 devices: a whole 2x2x4 slice. The times are simulated.
32 devices in a mesh: snp: 8 (over z, y), probe: 4 (over x, core).
Axes of the slice: x: 2, y: 2, z: 4, core: 2. Of those that a mesh axis runs over, the one named last changes fastest.
Arguments:
- dosage: bfloat16 [256, 16384], P(None, 'snp'), may hold values from 0 to 2, as said below
- allele_freq: float32 [16384], P('snp'), may hold values from 0.05 to 0.5
- probes: bfloat16 [32, 256], P('probe'), may hold values from -1 to 1, as said below
Outputs:
- kin_twice: float32 [32, 256], P('probe', 'snp')
- forms: float32 [2, 32], P(None, 'probe')
- estimates: float32 [2], replicated
Inputs may be any that keep to these rules, and one draw needn't show every extreme that they name: `dosage`: whole dosages. `probes`: every entry is -1 or 1.
All inputs are finite; a program needn't handle non-finite values.
Results may differ from a plain program's by a relative error of at most 0.0032.
Values may be sent and summed in bfloat16 or wider, within the bound.
No kernel may reach another device: no remote copies, remote signals or barrier semaphores. Data moves between devices by JAX's collectives and lax.ppermute only.
A program may use at most 64 MiB of HBM per device.

v0:
```python
import jax
import jax.numpy as jnp
from jax import lax
from jax.sharding import PartitionSpec as P


def apply_columns(vectors, standard):
    projected = jnp.dot(vectors, standard, preferred_element_type=jnp.float32).astype(jnp.bfloat16)
    return lax.dot_general(
        projected, standard, (((1,), (1,)), ((), ())), preferred_element_type=jnp.float32
    )


def body(dosage, allele_freq, probes):
    snp_count = lax.axis_size("snp")
    columns = dosage.shape[1] * snp_count
    owned = dosage.shape[0] // snp_count
    samples_all = dosage.shape[0]
    probes_all = probes.shape[0] * lax.axis_size("probe")
    scaling = lax.rsqrt(2.0 * allele_freq * (1.0 - allele_freq))
    standard = ((dosage.astype(jnp.float32) - 2.0 * allele_freq) * scaling).astype(jnp.bfloat16)
    start = lax.axis_index("snp") * owned
    signs_owned = lax.dynamic_slice_in_dim(probes, start, owned, 1).astype(jnp.float32)
    partial_once = apply_columns(probes, standard)
    summed = lax.psum(partial_once, "snp") / columns
    kin_owned = lax.dynamic_slice_in_dim(summed, start, owned, 1)
    kin_round = summed.astype(jnp.bfloat16)
    local_first = jnp.sum(signs_owned * kin_owned, axis=1) / samples_all
    form_first = lax.psum(local_first, "snp")
    partial_twice = apply_columns(kin_round, standard)
    kin_twice = lax.psum_scatter(partial_twice, "snp", scatter_dimension=1, tiled=True) / columns
    local_second = jnp.sum(signs_owned * kin_twice, axis=1) / samples_all
    form_second = lax.psum(local_second, "snp")
    forms = jnp.stack([form_first, form_second])
    estimates = lax.psum(jnp.sum(forms, axis=1), "probe") / probes_all
    return (kin_twice, forms, estimates)


def solution(mesh):
    placed = (P(None, "snp"), P("snp"), P("probe", None))
    return jax.shard_map(
        body,
        mesh=mesh,
        in_specs=placed,
        out_specs=(P("probe", "snp"), P(None, "probe"), P()),
        check_vma=False,
    )
```

profile of v0, /device:TPU:0, one launch (start us, length us, event | category | flops | bytes accessed | tf_op | source)
XLA Modules:
  0.0 129.7 jit_solution(3306518735828132539)
XLA Ops:
  7.2 0.0 reduce-scatter.4.cloned.1.call-start
  7.2 0.7 broadcast_multiply_fusion.1
  7.9 0.0 copy-start.1
  7.9 2.6 %fusion = f32[8,256]{1,0:T(8,128)S(1)} fusion(bf16[8,256]{1,0:T(8,128)(2,1)} %param.5, bf16[256,2048]{1,0:T(8,128)(2,1)} %param.3, f32[2048]{0:T(1024)S(1)} %get-tuple-element.11, f32[2048]{0:T(1024)S(1)} %get-tuple-element.10), kind=kOutput, calls=%fused_computation.3 | convolution fusion | flops 20987904 | bytes 1077248 | tf_op jit(solution)/shard_map/dot_general | solution.py:9
  10.5 23.4 %psum.28 = f32[8,256]{1,0:T(8,128)S(1)} all-reduce(f32[8,256]{1,0:T(8,128)S(1)} %fusion), channel_id=1, replica_groups=mesh['snp'=8,'probe'=4] {'snp'}, use_global_device_ids=true, to_apply=%region_0.0 | all-reduce | flops 2048 | bytes 16384 | tf_op jit(solution)/shard_map/psum | solution.py:25
  34.0 0.0 copy-done.1
  34.0 0.0 copy-start
  34.0 1.3 %convolution_bitcast_fusion = f32[256,8]{1,0:T(8,128)} fusion(bf16[256,2048]{1,0:T(8,128)(2,1)S(1)} %copy-done.1, f32[2048]{0:T(1024)S(1)} %get-tuple-element.11, f32[2048]{0:T(1024)S(1)} %get-tuple-element.10, f32[8,256]{1,0:T(8,128)S(1)} %psum.28), kind=kOutput, calls=%fused_computation.4 | convolution fusion | flops 20992000 | bytes 1081344
  35.3 0.0 reduce-scatter.4.cloned.1.call-update
  35.3 59.6 %reduce-scatter.4.cloned.1.call-done = f32[32,8]{1,0:T(8,128)} async-done(((f32[256,8]{1,0:T(8,128)}), f32[32,8]{1,0:T(8,128)}) %reduce-scatter.4.cloned.1.call-update) | async-done | bytes 1040
  95.0 0.8 copy.7
  95.7 0.0 copy-done
  95.7 0.7 fusion.1
  96.5 19.5 %all-reduce = (f32[1,8]{1,0:T(1,128)S(1)}, f32[1,8]{1,0:T(1,128)S(1)}) all-reduce(f32[1,8]{1,0:T(1,128)S(1)} %get-tuple-element.12, f32[1,8]{1,0:T(1,128)S(1)} %get-tuple-element.13), channel_id=1, replica_groups=mesh['snp'=8,'probe'=4] {'snp'}, use_global_device_ids=true, to_apply=%region_5.0 | all-reduce | flops 16 | bytes 128 | tf_op jit(solution)/shard_map/psum | solution.py:33
  116.0 0.7 fusion.5
  116.7 5.7 %psum.31 = f32[2]{0:T(128)S(1)} all-reduce(f32[2]{0:T(128)S(1)} %get-tuple-element.7), channel_id=1, replica_groups=mesh['snp'=8,'probe'=4] {'probe'}, use_global_device_ids=true, to_apply=%region_7.0 | all-reduce | flops 2 | bytes 16 | tf_op jit(solution)/shard_map/psum | solution.py:35
  122.4 0.5 broadcast_multiply_fusion.3
  (2 shorter events, 0.0 us)
Async XLA Ops:
  7.2 87.8 %reduce-scatter.4.cloned.1.call-start = ((), (), s32[]{:S(2)}) async-start(), calls=%async_computation.1 | async-start | bytes 147456
  7.9 26.0 %copy-start.1 = (bf16[256,2048]{1,0:T(8,128)(2,1)S(1)}, bf16[256,2048]{1,0:T(8,128)(2,1)}, u32[]{:S(2)}) copy-start(bf16[256,2048]{1,0:T(8,128)(2,1)} %param.3) | copy-start | bytes 3145732
  34.0 61.8 %copy-start = (bf16[8,256]{1,0:T(8,128)(2,1)S(1)}, bf16[8,256]{1,0:T(8,128)(2,1)}, u32[]{:S(2)}) copy-start(bf16[8,256]{1,0:T(8,128)(2,1)} %param.5) | copy-start | bytes 12292
Sparse Core Ops, SparseCore 0:
  35.4 59.4 reduce-scatter.3
where the time goes:
time: 130 us
  waiting for transfers between devices  59.6 us (46%)
  blocking collectives  48.6 us (37%)
  between operations  14.1 us (11%)
  matrix products  3.96 us (3%)
  other arithmetic  2.65 us (2%)
    unnamed x2, waiting for transfers between devices  59.6 us
    psum x1, blocking collectives, body(): summed = lax.psum(partial_once, 'snp') / columns  23.4 us
    psum x1, blocking collectives, body(): form_second = lax.psum(local_second, 'snp')  19.5 us
    psum x1, blocking collectives, body(): estimates = lax.psum(jnp.sum(forms, axis=1), 'probe') / probes_all  5.66 us
    dot_general x1, matrix products, apply_columns(): lax.dot_general(projected, standard, (((1,), (1,)), ((), ())), preferred_...  2.63 us
  transfers between devices with their start and end apart: 1, of which 1 were waited for; matrix products, arithmetic and copies ran while one was open for 0% of the time, Pallas kernels for 0%

commit v1 on v0

v1 whole, which is shorter than its diff:
```python
import jax
import jax.numpy as jnp
from jax import lax
from jax.sharding import PartitionSpec as P

BOTH = ("snp", "probe")


def body(dosage, allele_freq, probes):
    snp_count = lax.axis_size("snp")
    probe_count = lax.axis_size("probe")
    columns = dosage.shape[1] * snp_count
    samples = dosage.shape[0]
    rows = probes.shape[0]
    part = samples // (snp_count * probe_count)
    group = lax.axis_index("probe")
    scaling = lax.rsqrt(2.0 * allele_freq * (1.0 - allele_freq))
    standard = ((dosage.astype(jnp.float32) - 2.0 * allele_freq) * scaling).astype(jnp.bfloat16)
    across = (((1,), (1,)), ((), ()))
    mine = standard.reshape(snp_count, probe_count, part, -1)
    mine = lax.dynamic_index_in_dim(mine, group, 1, keepdims=False).reshape(snp_count * part, -1)
    projected = jnp.dot(probes, standard, preferred_element_type=jnp.float32).astype(jnp.bfloat16)
    left = jnp.concatenate([projected, mine], axis=0)
    partial = lax.dot_general(left, standard, across, preferred_element_type=jnp.float32) / columns
    signs = probes.astype(jnp.float32)
    signed = (signs * partial[:rows]).astype(jnp.bfloat16)
    kinship = partial[rows:].astype(jnp.bfloat16).reshape(snp_count, 1, part, samples)
    shape = (snp_count, probe_count)
    send = jnp.concatenate(
        [
            jnp.broadcast_to(signed, shape + (rows, samples)),
            jnp.broadcast_to(kinship, shape + (part, samples)),
        ],
        axis=2,
    ).reshape(snp_count * probe_count, rows + part, samples)
    got = lax.all_to_all(send, BOTH, 0, 0, tiled=True)
    summed = jnp.sum(got.reshape(shape + (rows + part, samples)).astype(jnp.float32), axis=0)
    signed_all = summed[:, :rows]
    kinship_owned = summed[:, rows:].reshape(probe_count * part, samples)
    rounded_all = lax.reduce_precision(signed_all, 8, 7)
    first = jnp.sum(signed_all, axis=2) / samples
    second = jnp.sum(rounded_all * signed_all, axis=2) / samples
    both = jnp.stack([first, second])
    estimates = jnp.sum(both, axis=(1, 2)) / (rows * probe_count)
    forms = lax.dynamic_index_in_dim(both, group, 1, keepdims=False)
    kin_round = signs * lax.dynamic_index_in_dim(rounded_all, group, 0, keepdims=False)
    kin_twice = lax.dot_general(
        kin_round, kinship_owned, across, precision=lax.Precision.HIGHEST,
        preferred_element_type=jnp.float32,
    )
    return (kin_twice, forms, estimates)


def solution(mesh):
    placed = (P(None, "snp"), P("snp"), P("probe", None))
    return jax.shard_map(
        body,
        mesh=mesh,
        in_specs=placed,
        out_specs=(P("probe", "snp"), P(None, "probe"), P()),
        check_vma=False,
    )
```

time: 130 us -> 23.7 us (0.18)
  waiting for transfers between devices: 59.6 us -> 0 us
  blocking collectives: 48.6 us -> 17.7 us
  between operations: 14.1 us -> 0.7 us
  matrix products: 3.96 us -> 1.45 us
    unnamed x2 -> x0, waiting for transfers between devices: 59.6 us -> none
    psum x3 -> x0, blocking collectives: 48.6 us -> none  [the longest x1 23.4 us: body(): summed = lax.psum(partial_once, 'snp') / columns]
    all_to_all x0 -> x1, blocking collectives: none -> 17.7 us  [body(): got = lax.all_to_all(send, BOTH, 0, 0, tiled=True)]
    convert_element_type x0 -> x2, other arithmetic: none -> 1.51 us  [the longest x1 1.51 us: body(): ((dosage.astype(jnp.float32) - 2.0 * allele_freq) * scaling).astype(jnp.b...]
    unnamed x1 -> x0, matrix products: 1.32 us -> none
    dot_general x1 -> x3, matrix products: 2.63 us -> 1.45 us  [the longest x1 0.74 us: body(): lax.dot_general(kin_round, kinship_owned, across, precision=lax.Precision...]
  transfers between devices with their start and end apart: 1 -> 0, of which waited for: 1 -> 0; matrix products, arithmetic and copies ran while one was open for 0% -> 0% of each run, Pallas kernels for 0% -> 0%
where the time goes in v1:
time: 23.7 us; the launch traced here: 23.5 us
  blocking collectives  17.7 us (75%)
  other arithmetic  3.56 us (15%)
  matrix products  1.45 us (6%)
  between operations  0.7 us (3%)
    all_to_all x1, blocking collectives, body(): got = lax.all_to_all(send, BOTH, 0, 0, tiled=True)  17.7 us
    convert_element_type x1, other arithmetic, body(): ((dosage.astype(jnp.float32) - 2.0 * allele_freq) * scaling).astype(jnp.b...  1.51 us
    dot_general x1, matrix products, body(): lax.dot_general(kin_round, kinship_owned, across, precision=lax.Precision...  0.74 us
    mul x1, other arithmetic, body(): 2.0 * allele_freq  0.7 us
    another operation x1, other arithmetic, body(): both = jnp.stack([first, second])  0.58 us
    div x1, other arithmetic, body(): estimates = jnp.sum(both, axis=(1, 2)) / (rows * probe_count)  0.51 us

profile of v1, /device:TPU:0, one launch (start us, length us, event | category | flops | bytes accessed | tf_op | source)
XLA Modules:
  0.0 23.5 jit_solution(9322109358326664816)
XLA Ops:
  0.6 0.7 %broadcast_multiply_fusion = (f32[2048]{0:T(1024)S(1)}, f32[2048]{0:T(1024)S(1)}) fusion(f32[2048]{0:T(1024)} %param.4), kind=kLoop, calls=%fused_computation.27 | loop fusion | flops 6144 | bytes 24576 | tf_op jit(solution)/shard_map/mul | solution.py:18
  1.3 0.0 copy-start
  1.3 1.5 %multiply_convert_fusion = bf16[256,2048]{1,0:T(8,128)(2,1)S(1)} fusion(bf16[256,2048]{1,0:T(8,128)(2,1)} %param.3, f32[2048]{0:T(1024)S(1)} %get-tuple-element.7, f32[2048]{0:T(1024)S(1)} %get-tuple-element.6), kind=kLoop, calls=%fused_computation.2 | loop fusion | flops 2097152 | bytes 2113536 | tf_op jit(solution)/shard_map/convert_element_type | solution.py:18
  2.9 0.0 copy-done
  2.9 0.2 %fusion = bf16[8,2048]{1,0:T(8,128)(2,1)S(1)} fusion(bf16[256,2048]{1,0:T(8,128)(2,1)S(1)} %multiply_convert_fusion, bf16[8,256]{1,0:T(8,128)(2,1)S(1)} %copy-done), kind=kOutput, calls=%fused_computation.1 | convolution fusion | flops 8404992 | bytes 1085440 | tf_op jit(solution)/shard_map/dot_general | solution.py:22
  3.1 0.5 %convolution_multiply_fusion = f32[72,256]{1,0:T(8,128)S(1)} fusion(bf16[256,2048]{1,0:T(8,128)(2,1)S(1)} %multiply_convert_fusion, bf16[64,2048]{1,0:T(8,128)(2,1)S(1)} %dynamic-slice_bitcast_fusion, bf16[8,2048]{1,0:T(8,128)(2,1)S(1)} %fusion), kind=kOutput, calls=%fused_computation.3 | convolution fusion | flops 76105728 | bytes 1417216 | tf_op jit(solution)/shard_map/dot_general | solution.py:24
  3.7 17.7 %all_to_all.5 = bf16[32,16,256]{2,1,0:T(8,128)(2,1)S(1)} all-to-all(bf16[32,16,256]{2,1,0:T(8,128)(2,1)S(1)} %bitcast.28), channel_id=1, replica_groups=mesh['snp'=8,'probe'=4] {'snp','probe'}, dimensions={0} | all-to-all | bytes 524288 | tf_op jit(solution)/shard_map/all_to_all | solution.py:36
  21.4 0.1 multiply_reduce_fusion
  21.5 0.6 %fusion.10 = f32[2,1,8]{2,1,0:T(1,128)} fusion(s32[]{:T(128)S(6)} %select_n.8, f32[1,4,8]{2,1,0:T(4,128)S(1)} %get-tuple-element.9, f32[1,4,8]{2,1,0:T(4,128)S(1)} %get-tuple-element.8), kind=kLoop, calls=%fused_computation.30 | loop fusion | flops 16 | bytes 324 | tf_op jit(solution)/shard_map/stack | solution.py:43
  22.1 0.1 fusion.9
  22.2 0.7 %fusion.5 = f32[8,32]{1,0:T(8,128)} fusion(f32[4,16,256]{2,1,0:T(8,128)S(1)} %convert_reduce_fusion, bf16[8,256]{1,0:T(8,128)(2,1)S(1)} %copy-done, f32[4,8,256]{2,1,0:T(8,128)S(1)} %get-tuple-element.5, s32[]{:T(128)S(6)} %select_n.8), kind=kOutput, calls=%fused_computation.13 | convolution fusion | flops 790528 | bytes 46084 | tf_op jit(solution)/shard_map/dot_general | solution.py:47
  23.0 0.5 %broadcast_multiply_fusion.1 = f32[2]{0:T(128)} fusion(f32[2]{0:T(128)S(1)} %fusion.9), kind=kLoop, calls=%fused_computation.32 | loop fusion | flops 2 | bytes 16 | tf_op jit(solution)/shard_map/div | solution.py:44
  (8 shorter events, 0.1 us)
Async XLA Ops:
  1.3 1.5 %copy-start = (bf16[8,256]{1,0:T(8,128)(2,1)S(1)}, bf16[8,256]{1,0:T(8,128)(2,1)}, u32[]{:S(2)}) copy-start(bf16[8,256]{1,0:T(8,128)(2,1)} %param.5) | copy-start | bytes 12292

commit v2 on v0

v2 whole, which is shorter than its diff:
```python
import functools

import jax
import jax.numpy as jnp
from jax import lax
from jax.experimental import pallas as pl
from jax.experimental.pallas import tpu as pltpu
from jax.sharding import PartitionSpec as P

BOTH = ("snp", "probe")
ACROSS = (((1,), (1,)), ((), ()))
CHUNKS = 4


def first_kernel(
    dosage, freq_hbm, probes_hbm, send, stage, freq, probes, sems, *, snp_count, probe_count, columns
):
    samples, width = dosage.shape
    rows = probes.shape[0]
    part = samples // (snp_count * probe_count)
    step = width // CHUNKS
    copies = [
        pltpu.make_async_copy(dosage.at[:, pl.ds(c * step, step)], stage.at[c], sems.at[c])
        for c in range(CHUNKS)
    ]
    small = [
        pltpu.make_async_copy(freq_hbm, freq, sems.at[CHUNKS]),
        pltpu.make_async_copy(probes_hbm, probes, sems.at[CHUNKS + 1]),
    ]
    for copy in small + copies:
        copy.start()
    group = lax.axis_index("probe")
    row = lax.broadcasted_iota(jnp.int32, (snp_count * part, samples), 0)
    col = lax.broadcasted_iota(jnp.int32, (snp_count * part, samples), 1)
    owner = row // part
    wanted = owner * (part * probe_count) + group * part + (row - owner * part)
    pick = jnp.where(col == wanted, 1.0, 0.0).astype(jnp.bfloat16)
    for copy in small:
        copy.wait()
    signs = probes[...]
    left = jnp.concatenate([signs, pick], axis=0)
    total = jnp.zeros((left.shape[0], samples), jnp.float32)
    for c in range(CHUNKS):
        f = freq[:, c * step : (c + 1) * step]
        mean = 2.0 * f
        scaling = lax.rsqrt(mean * (1.0 - f))
        copies[c].wait()
        standard = ((stage[c].astype(jnp.float32) - mean) * scaling).astype(jnp.bfloat16)
        projected = jnp.dot(left, standard, preferred_element_type=jnp.float32)
        total = total + lax.dot_general(
            projected.astype(jnp.bfloat16), standard, ACROSS, preferred_element_type=jnp.float32
        )
    total = total * (1.0 / columns)
    signed = (signs.astype(jnp.float32) * total[:rows]).astype(jnp.bfloat16)
    kinship = total[rows:].astype(jnp.bfloat16)
    for i in range(snp_count):
        block = jnp.concatenate([signed, kinship[i * part : (i + 1) * part]], axis=0)
        for q in range(probe_count):
            send[i * probe_count + q] = block


def second_kernel(got, probes, kin_twice, forms, estimates, sums, *, snp_count, probe_count):
    rows, samples = probes.shape
    part = got.shape[1] - rows
    group = lax.axis_index("probe")
    for q in range(probe_count):
        summed = got[q].astype(jnp.float32)
        for j in range(1, snp_count):
            summed = summed + got[j * probe_count + q].astype(jnp.float32)
        sums[q] = summed
    everyone = sums[:, :rows]
    rounded = everyone.astype(jnp.bfloat16)
    scale = 1.0 / samples
    first_all = jnp.sum(everyone) * scale
    second_all = jnp.sum(rounded.astype(jnp.float32) * everyone) * scale
    mean = 1.0 / (rows * probe_count)
    lane = lax.broadcasted_iota(jnp.int32, (1, 2), 1)
    estimates[...] = jnp.where(lane == 0, first_all, second_all) * mean
    mine = sums[group][:rows]
    mine_round = mine.astype(jnp.bfloat16)
    first = jnp.sum(mine, axis=1, keepdims=True) * scale
    second = jnp.sum(mine_round.astype(jnp.float32) * mine, axis=1, keepdims=True) * scale
    at = lax.broadcasted_iota(jnp.int32, (rows, rows), 0)
    on = at == lax.broadcasted_iota(jnp.int32, (rows, rows), 1)
    forms[0:1] = jnp.sum(jnp.where(on, first, 0.0), axis=0, keepdims=True)
    forms[1:2] = jnp.sum(jnp.where(on, second, 0.0), axis=0, keepdims=True)
    kinship = sums[:, rows:].reshape(probe_count * part, samples)
    high = kinship.astype(jnp.bfloat16)
    low = (kinship - high.astype(jnp.float32)).astype(jnp.bfloat16)
    vectors = probes[...] * mine_round
    kin_twice[...] = lax.dot_general(
        vectors, high, ACROSS, preferred_element_type=jnp.float32
    ) + lax.dot_general(vectors, low, ACROSS, preferred_element_type=jnp.float32)


def body(dosage, allele_freq, probes):
    snp_count = lax.axis_size("snp")
    probe_count = lax.axis_size("probe")
    samples, width = dosage.shape
    rows = probes.shape[0]
    devices = snp_count * probe_count
    part = samples // devices
    vmem = pl.BlockSpec(memory_space=pltpu.VMEM)
    hbm = pl.BlockSpec(memory_space=pltpu.HBM)
    stay = functools.partial(pltpu.with_memory_space_constraint, memory_space=pltpu.HBM)
    params = pltpu.CompilerParams(vmem_limit_bytes=min(56 << 20, max(16 << 20, 16 * samples * width)))
    send = pl.pallas_call(
        functools.partial(
            first_kernel, snp_count=snp_count, probe_count=probe_count, columns=width * snp_count
        ),
        in_specs=[hbm, hbm, hbm],
        out_specs=vmem,
        out_shape=jax.ShapeDtypeStruct((devices, rows + part, samples), jnp.bfloat16),
        scratch_shapes=[
            pltpu.VMEM((CHUNKS, samples, width // CHUNKS), jnp.bfloat16),
            pltpu.VMEM((1, width), jnp.float32),
            pltpu.VMEM((rows, samples), jnp.bfloat16),
            pltpu.SemaphoreType.DMA((CHUNKS + 2,)),
        ],
        compiler_params=params,
        name="first",
    )(*(stay(x) for x in (dosage, allele_freq.reshape(1, width), probes)))
    got = lax.all_to_all(send, BOTH, 0, 0, tiled=True)
    kin_twice, forms, estimates = pl.pallas_call(
        functools.partial(second_kernel, snp_count=snp_count, probe_count=probe_count),
        in_specs=[vmem, vmem],
        out_specs=[vmem, vmem, vmem],
        out_shape=[
            jax.ShapeDtypeStruct((rows, samples // snp_count), jnp.float32),
            jax.ShapeDtypeStruct((2, rows), jnp.float32),
            jax.ShapeDtypeStruct((1, 2), jnp.float32),
        ],
        scratch_shapes=[pltpu.VMEM((probe_count, rows + part, samples), jnp.float32)],
        compiler_params=params,
        name="second",
    )(got, probes)
    return (kin_twice, forms, estimates.reshape(2))


def solution(mesh):
    placed = (P(None, "snp"), P("snp"), P("probe", None))
    return jax.shard_map(
        body,
        mesh=mesh,
        in_specs=placed,
        out_specs=(P("probe", "snp"), P(None, "probe"), P()),
        check_vma=False,
    )
```

time: 130 us -> 21.6 us (0.17)
  waiting for transfers between devices: 59.6 us -> 0 us
  blocking collectives: 48.6 us -> 17.7 us
  between operations: 14.1 us -> 0.65 us
  matrix products: 3.96 us -> 0 us
  Pallas kernels: 0 us -> 3.05 us
  other arithmetic: 2.65 us -> 0 us
    unnamed x2 -> x0, waiting for transfers between devices: 59.6 us -> none
    psum x3 -> x0, blocking collectives: 48.6 us -> none  [the longest x1 23.4 us: body(): summed = lax.psum(partial_once, 'snp') / columns]
    all_to_all x0 -> x1, blocking collectives: none -> 17.7 us  [body(): got = lax.all_to_all(send, BOTH, 0, 0, tiled=True)]
    pallas_call x0 -> x2, Pallas kernels: none -> 3.05 us  [the longest x1 2.29 us: body(): pl.pallas_call(functools.partial(first_kernel, snp_count=snp_count, probe...]
    dot_general x1 -> x0, matrix products: 2.63 us -> none  [apply_columns(): lax.dot_general(projected, standard, (((1,), (1,)), ((), ())), preferred_...]
    reduce_sum x2 -> x0, other arithmetic: 1.42 us -> none  [the longest x1 0.74 us: body(): local_first = jnp.sum(signs_owned * kin_owned, axis=1) / samples_all]
    unnamed x1 -> x0, matrix products: 1.32 us -> none
  transfers between devices with their start and end apart: 1 -> 0, of which waited for: 1 -> 0; matrix products, arithmetic and copies ran while one was open for 0% -> 0% of each run, Pallas kernels for 0% -> 0%
where the time goes in v2:
time: 21.6 us; the launch traced here: 21.4 us
  blocking collectives  17.7 us (82%)
  Pallas kernels  3.05 us (14%)
  between operations  0.65 us (3%)
    all_to_all x1, blocking collectives, body(): got = lax.all_to_all(send, BOTH, 0, 0, tiled=True)  17.7 us
    pallas_call x1, Pallas kernels, body(): pl.pallas_call(functools.partial(first_kernel, snp_count=snp_count, probe...  2.29 us
    pallas_call x1, Pallas kernels, body(): pl.pallas_call(functools.partial(second_kernel, snp_count=snp_count, prob...  0.76 us

profile of v2, /device:TPU:0, one launch (start us, length us, event | category | flops | bytes accessed | tf_op | source)
XLA Modules:
  0.0 21.4 jit_solution(7772861083948820908)
XLA Ops:
  0.6 2.3 %first.1 = bf16[32,16,256]{2,1,0:T(8,128)(2,1)S(1)} custom-call(bf16[256,2048]{1,0:T(8,128)(2,1)} %dosage.1, f32[1,2048]{1,0:T(1,128)} %bitcast.2, bf16[8,256]{1,0:T(8,128)(2,1)} %probes.1), custom_call_target="tpu_custom_call" | custom-call | tf_op jit(solution)/shard_map/first/pallas_call | solution.py:107
  2.9 0.0 copy-start
  2.9 17.7 %all_to_all.5.got = bf16[32,16,256]{2,1,0:T(8,128)(2,1)S(1)} all-to-all(bf16[32,16,256]{2,1,0:T(8,128)(2,1)S(1)} %first.1), channel_id=1, replica_groups=mesh['snp'=8,'probe'=4] {'snp','probe'}, dimensions={0} | all-to-all | bytes 524288 | tf_op jit(solution)/shard_map/all_to_all | solution.py:123
  20.6 0.0 copy-done
  20.6 0.8 %second.1 = (f32[8,32]{1,0:T(8,128)}, f32[2,8]{1,0:T(2,128)}, f32[1,2]{1,0:T(1,128)}) custom-call(bf16[32,16,256]{2,1,0:T(8,128)(2,1)S(1)} %all_to_all.5.got, bf16[8,256]{1,0:T(8,128)(2,1)S(1)} %copy-done), custom_call_target="tpu_custom_call" | custom-call | tf_op jit(solution)/shard_map/second/pallas_call | solution.py:124
Async XLA Ops:
  2.9 17.7 %copy-start = (bf16[8,256]{1,0:T(8,128)(2,1)S(1)}, bf16[8,256]{1,0:T(8,128)(2,1)}, u32[]{:S(2)}) copy-start(bf16[8,256]{1,0:T(8,128)(2,1)} %probes.1) | copy-start | bytes 12292

commit v3 on v2

--- a/solution.py
+++ b/solution.py
@@ -53,44 +53,72 @@
     total = total * (1.0 / columns)
     signed = (signs.astype(jnp.float32) * total[:rows]).astype(jnp.bfloat16)
     kinship = total[rows:].astype(jnp.bfloat16)
+    half = samples // 2
     for i in range(snp_count):
         block = jnp.concatenate([signed, kinship[i * part : (i + 1) * part]], axis=0)
         for q in range(probe_count):
-            send[i * probe_count + q] = block
+            send[i * probe_count + q] = block[:, (q % 2) * half : (q % 2 + 1) * half]
 
 
-def second_kernel(got, probes, kin_twice, forms, estimates, sums, *, snp_count, probe_count):
-    rows, samples = probes.shape
+def sum_kernel(got, share, own, sums, *, snp_count, probe_count, rows):
     part = got.shape[1] - rows
+    owned = part * probe_count
     group = lax.axis_index("probe")
+    partner = group + 1 - 2 * (group % 2)
+    first = jnp.zeros((rows, got.shape[2]), jnp.float32)
+    second = first
     for q in range(probe_count):
         summed = got[q].astype(jnp.float32)
         for j in range(1, snp_count):
             summed = summed + got[j * probe_count + q].astype(jnp.float32)
-        sums[q] = summed
-    everyone = sums[:, :rows]
-    rounded = everyone.astype(jnp.bfloat16)
+        signed = summed[:rows]
+        sums[q] = signed
+        share[q * part : (q + 1) * part] = summed[rows:]
+        first = first + signed
+        second = second + signed.astype(jnp.bfloat16).astype(jnp.float32) * signed
+    share[owned : owned + rows] = first
+    share[owned + rows : owned + 2 * rows] = second
+    share[owned + 2 * rows :] = sums[partner]
+    own[...] = sums[group]
+
+
+def last_kernel(share, other, own, probes, kin_twice, forms, estimates, *, probe_count):
+    rows, samples = probes.shape
+    half = samples // 2
+    owned = share.shape[0] - 3 * rows
+    low_half = lax.axis_index("probe") % 2 == 0
     scale = 1.0 / samples
-    first_all = jnp.sum(everyone) * scale
-    second_all = jnp.sum(rounded.astype(jnp.float32) * everyone) * scale
-    mean = 1.0 / (rows * probe_count)
+    mean = scale / (rows * probe_count)
+    ends = share[owned : owned + 2 * rows] + other[owned : owned + 2 * rows]
     lane = lax.broadcasted_iota(jnp.int32, (1, 2), 1)
-    estimates[...] = jnp.where(lane == 0, first_all, second_all) * mean
-    mine = sums[group][:rows]
-    mine_round = mine.astype(jnp.bfloat16)
-    first = jnp.sum(mine, axis=1, keepdims=True) * scale
-    second = jnp.sum(mine_round.astype(jnp.float32) * mine, axis=1, keepdims=True) * scale
+    estimates[...] = jnp.where(lane == 0, jnp.sum(ends[:rows]), jnp.sum(ends[rows:])) * mean
+    signs = probes[...].astype(jnp.float32)
+    signs_low = signs[:, :half]
+    signs_high = signs[:, half:]
+    first = jnp.zeros((rows, half), jnp.float32)
+    second = first
+    twice = jnp.zeros((rows, owned), jnp.float32)
+    for signed, rest, sign in (
+        (own[...], share, jnp.where(low_half, signs_low, signs_high)),
+        (other[owned + 2 * rows :], other, jnp.where(low_half, signs_high, signs_low)),
+    ):
+        rounded = signed.astype(jnp.bfloat16).astype(jnp.float32)
+        first = first + signed
+        second = second + rounded * signed
+        vectors = (sign * rounded).astype(jnp.bfloat16)
+        kinship = rest[:owned]
+        high = kinship.astype(jnp.bfloat16)
+        low = (kinship - high.astype(jnp.float32)).astype(jnp.bfloat16)
+        for piece in (high, low):
+            twice = twice + lax.dot_general(
+                vectors, piece, ACROSS, preferred_element_type=jnp.float32
+            )
+    kin_twice[...] = twice
     at = lax.broadcasted_iota(jnp.int32, (rows, rows), 0)
     on = at == lax.broadcasted_iota(jnp.int32, (rows, rows), 1)
-    forms[0:1] = jnp.sum(jnp.where(on, first, 0.0), axis=0, keepdims=True)
-    forms[1:2] = jnp.sum(jnp.where(on, second, 0.0), axis=0, keepdims=True)
-    kinship = sums[:, rows:].reshape(probe_count * part, samples)
-    high = kinship.astype(jnp.bfloat16)
-    low = (kinship - high.astype(jnp.float32)).astype(jnp.bfloat16)
-    vectors = probes[...] * mine_round
-    kin_twice[...] = lax.dot_general(
-        vectors, high, ACROSS, preferred_element_type=jnp.float32
-    ) + lax.dot_general(vectors, low, ACROSS, preferred_element_type=jnp.float32)
+    for k, form in enumerate((first, second)):
+        total = jnp.sum(form, axis=1, keepdims=True) * scale
+        forms[k : k + 1] = jnp.sum(jnp.where(on, total, 0.0), axis=0, keepdims=True)
 
 
 def body(dosage, allele_freq, probes):
@@ -100,6 +128,8 @@
     rows = probes.shape[0]
     devices = snp_count * probe_count
     part = samples // devices
+    half = samples // 2
+    owned = samples // snp_count
     vmem = pl.BlockSpec(memory_space=pltpu.VMEM)
     hbm = pl.BlockSpec(memory_space=pltpu.HBM)
     stay = functools.partial(pltpu.with_memory_space_constraint, memory_space=pltpu.HBM)
@@ -110,7 +140,7 @@
         ),
         in_specs=[hbm, hbm, hbm],
         out_specs=vmem,
-        out_shape=jax.ShapeDtypeStruct((devices, rows + part, samples), jnp.bfloat16),
+        out_shape=jax.ShapeDtypeStruct((devices, rows + part, half), jnp.bfloat16),
         scratch_shapes=[
             pltpu.VMEM((CHUNKS, samples, width // CHUNKS), jnp.bfloat16),
             pltpu.VMEM((1, width), jnp.float32),
@@ -121,19 +151,31 @@
         name="first",
     )(*(stay(x) for x in (dosage, allele_freq.reshape(1, width), probes)))
     got = lax.all_to_all(send, BOTH, 0, 0, tiled=True)
+    share, own = pl.pallas_call(
+        functools.partial(sum_kernel, snp_count=snp_count, probe_count=probe_count, rows=rows),
+        in_specs=[vmem],
+        out_specs=[vmem, vmem],
+        out_shape=[
+            jax.ShapeDtypeStruct((owned + 3 * rows, half), jnp.float32),
+            jax.ShapeDtypeStruct((rows, half), jnp.float32),
+        ],
+        scratch_shapes=[pltpu.VMEM((probe_count, rows, half), jnp.float32)],
+        compiler_params=params,
+        name="sums",
+    )(got)
+    other = lax.ppermute(share, "probe", [(q, q ^ 1) for q in range(probe_count)])
     kin_twice, forms, estimates = pl.pallas_call(
-        functools.partial(second_kernel, snp_count=snp_count, probe_count=probe_count),
-        in_specs=[vmem, vmem],
+        functools.partial(last_kernel, probe_count=probe_count),
+        in_specs=[vmem, vmem, vmem, vmem],
         out_specs=[vmem, vmem, vmem],
         out_shape=[
-            jax.ShapeDtypeStruct((rows, samples // snp_count), jnp.float32),
+            jax.ShapeDtypeStruct((rows, owned), jnp.float32),
             jax.ShapeDtypeStruct((2, rows), jnp.float32),
             jax.ShapeDtypeStruct((1, 2), jnp.float32),
         ],
-        scratch_shapes=[pltpu.VMEM((probe_count, rows + part, samples), jnp.float32)],
         compiler_params=params,
-        name="second",
-    )(got, probes)
+        name="last",
+    )(share, other, own, probes)
     return (kin_twice, forms, estimates.reshape(2))
 
 

time: 21.6 us -> 20.5 us (0.949)
  blocking collectives: 17.7 us -> 15.3 us
  waiting for transfers between devices: 0 us -> 0.99 us
  starting transfers between devices: 0 us -> 0.28 us
    all_to_all x1, blocking collectives: 17.7 us -> 15.3 us  [body(): got = lax.all_to_all(send, BOTH, 0, 0, tiled=True)]
    ppermute x0 -> x1, waiting for transfers between devices: none -> 0.99 us  [body(): lax.ppermute(share, 'probe', [(q, q ^ 1) for q in range(probe_count)])]
    ppermute x0 -> x1, starting transfers between devices: none -> 0.28 us  [body(): lax.ppermute(share, 'probe', [(q, q ^ 1) for q in range(probe_count)])]
    pallas_call x1 -> x2, Pallas kernels: 0.76 us -> 0.76 us  [the longest x1 0.73 us: body(): pl.pallas_call(functools.partial(last_kernel, probe_count=probe_count), i...]
  transfers between devices with their start and end apart: 0 -> 1, of which waited for: 0 -> 1; matrix products, arithmetic and copies ran while one was open for 0% -> 0% of each run, Pallas kernels for 0% -> 0%
where the time goes in v3:
time: 20.5 us; the launch traced here: 20.3 us
  blocking collectives  15.3 us (75%)
  Pallas kernels  3.05 us (15%)
  waiting for transfers between devices  0.99 us (5%)
  between operations  0.64 us (3%)
  starting transfers between devices  0.28 us (1%)
    all_to_all x1, blocking collectives, body(): got = lax.all_to_all(send, BOTH, 0, 0, tiled=True)  15.3 us
    pallas_call x1, Pallas kernels, body(): pl.pallas_call(functools.partial(first_kernel, snp_count=snp_count, probe...  2.29 us
    ppermute x1, waiting for transfers between devices, body(): lax.ppermute(share, 'probe', [(q, q ^ 1) for q in range(probe_count)])  0.99 us
    pallas_call x1, Pallas kernels, body(): pl.pallas_call(functools.partial(last_kernel, probe_count=probe_count), i...  0.73 us
  transfers between devices with their start and end apart: 1, of which 1 were waited for; matrix products, arithmetic and copies ran while one was open for 0% of the time, Pallas kernels for 0%

profile of v3, /device:TPU:0, one launch (start us, length us, event | category | flops | bytes accessed | tf_op | source)
XLA Modules:
  0.0 20.3 jit_solution(11251421142862577778)
XLA Ops:
  0.6 2.3 %first.1 = bf16[32,16,128]{2,1,0:T(8,128)(2,1)S(1)} custom-call(bf16[256,2048]{1,0:T(8,128)(2,1)} %dosage.1, f32[1,2048]{1,0:T(1,128)} %bitcast.2, bf16[8,256]{1,0:T(8,128)(2,1)} %probes.1), custom_call_target="tpu_custom_call" | custom-call | tf_op jit(solution)/shard_map/first/pallas_call | solution.py:137
  2.9 15.3 %all_to_all.5.got = bf16[32,16,128]{2,1,0:T(8,128)(2,1)S(1)} all-to-all(bf16[32,16,128]{2,1,0:T(8,128)(2,1)S(1)} %first.1), channel_id=1, replica_groups=mesh['snp'=8,'probe'=4] {'snp','probe'}, dimensions={0} | all-to-all | bytes 262144 | tf_op jit(solution)/shard_map/all_to_all | solution.py:153
  18.3 0.0 copy-start
  18.3 0.3 %collective-permute-start = (f32[56,128]{1,0:T(8,128)S(1)}, f32[56,128]{1,0:T(8,128)S(1)}, u32[]{:S(2)}, u32[]{:S(2)}) collective-permute-start(f32[56,128]{1,0:T(8,128)S(1)} %get-tuple-element.8.share), channel_id=1, source_target_pairs={{0,1},{1,0},{2,3},{3,2},{4,5},{5,4},{6,7},{7,6},{8,9},{9,8},{10,11... | collective-permute-start | bytes 86024 | tf_op jit(solution)/shard_map/ppermute | solution.py:166
  18.6 1.0 %collective-permute-done.other = f32[56,128]{1,0:T(8,128)S(1)} collective-permute-done((f32[56,128]{1,0:T(8,128)S(1)}, f32[56,128]{1,0:T(8,128)S(1)}, u32[]{:S(2)}, u32[]{:S(2)}) %collective-permute-start) | collective-permute-done | bytes 28704 | tf_op jit(solution)/shard_map/ppermute | solution.py:166
  19.6 0.0 copy-done
  19.6 0.7 %last.1 = (f32[8,32]{1,0:T(8,128)}, f32[2,8]{1,0:T(2,128)}, f32[1,2]{1,0:T(1,128)}) custom-call(f32[56,128]{1,0:T(8,128)S(1)} %get-tuple-element.8.share, f32[56,128]{1,0:T(8,128)S(1)} %collective-permute-done.other, f32[8,128]{1,0:T(8,128)S(1)} %get-tuple-element.9.own, bf16[8,256]{1,0:T(8,128)(2,1)S(1)} %copy-done), custom_call_target="tpu_custom_call" | custom-call | tf_op jit(solution)/shard_map/last/pallas_call | solution.py:167
  (1 shorter events, 0.0 us)
Async XLA Ops:
  18.3 1.3 %copy-start = (bf16[8,256]{1,0:T(8,128)(2,1)S(1)}, bf16[8,256]{1,0:T(8,128)(2,1)}, u32[]{:S(2)}) copy-start(bf16[8,256]{1,0:T(8,128)(2,1)} %probes.1) | copy-start | bytes 12292
  18.3 1.3 %collective-permute-start = (f32[56,128]{1,0:T(8,128)S(1)}, f32[56,128]{1,0:T(8,128)S(1)}, u32[]{:S(2)}, u32[]{:S(2)}) collective-permute-start(f32[56,128]{1,0:T(8,128)S(1)} %get-tuple-element.8.share), channel_id=1, source_target_pairs={{0,1},{1,0},{2,3},{3,2},{4,5},{5,4},{6,7},{7,6},{8,9},{9,8},{10,11... | collective-permute-start | bytes 86024 | tf_op jit(solution)/shard_map/ppermute | solution.py:166

commit v4 on v3

--- a/solution.py
+++ b/solution.py
@@ -9,7 +9,7 @@
 
 BOTH = ("snp", "probe")
 ACROSS = (((1,), (1,)), ((), ()))
-CHUNKS = 4
+CHUNKS = 2
 
 
 def first_kernel(
@@ -39,18 +39,25 @@
         copy.wait()
     signs = probes[...]
     left = jnp.concatenate([signs, pick], axis=0)
+    weight = jnp.sum(left.astype(jnp.float32), axis=1, keepdims=True)
+    mean = 2.0 * freq[...]
+    square = 1.0 / (mean * (1.0 - 0.5 * mean))
     total = jnp.zeros((left.shape[0], samples), jnp.float32)
+    shift = jnp.zeros((left.shape[0], step), jnp.float32)
     for c in range(CHUNKS):
-        f = freq[:, c * step : (c + 1) * step]
-        mean = 2.0 * f
-        scaling = lax.rsqrt(mean * (1.0 - f))
+        m = mean[:, c * step : (c + 1) * step]
         copies[c].wait()
-        standard = ((stage[c].astype(jnp.float32) - mean) * scaling).astype(jnp.bfloat16)
-        projected = jnp.dot(left, standard, preferred_element_type=jnp.float32)
-        total = total + lax.dot_general(
-            projected.astype(jnp.bfloat16), standard, ACROSS, preferred_element_type=jnp.float32
-        )
-    total = total * (1.0 / columns)
+        raw = jnp.dot(left, stage[c], preferred_element_type=jnp.float32)
+        if c:
+            total = total + lax.dot_general(
+                scaled, stage[c - 1], ACROSS, preferred_element_type=jnp.float32
+            )
+        scaled = ((raw - weight * m) * square[:, c * step : (c + 1) * step]).astype(jnp.bfloat16)
+        shift = shift + scaled.astype(jnp.float32) * m
+    total = total + lax.dot_general(
+        scaled, stage[CHUNKS - 1], ACROSS, preferred_element_type=jnp.float32
+    )
+    total = (total - jnp.sum(shift, axis=1, keepdims=True)) * (1.0 / columns)
     signed = (signs.astype(jnp.float32) * total[:rows]).astype(jnp.bfloat16)
     kinship = total[rows:].astype(jnp.bfloat16)
     half = samples // 2

time: 20.5 us -> 20.1 us (0.980)
  Pallas kernels: 3.05 us -> 2.64 us
    pallas_call x1, Pallas kernels: 2.29 us -> 1.88 us  [body(): pl.pallas_call(functools.partial(first_kernel, snp_count=snp_count, probe...]
where the time goes in v4:
time: 20.1 us; the launch traced here: 19.9 us
  blocking collectives  15.3 us (76%)
  Pallas kernels  2.64 us (13%)
  waiting for transfers between devices  0.99 us (5%)
  between operations  0.64 us (3%)
  starting transfers between devices  0.28 us (1%)
    all_to_all x1, blocking collectives, body(): got = lax.all_to_all(send, BOTH, 0, 0, tiled=True)  15.3 us
    pallas_call x1, Pallas kernels, body(): pl.pallas_call(functools.partial(first_kernel, snp_count=snp_count, probe...  1.88 us
    ppermute x1, waiting for transfers between devices, body(): lax.ppermute(share, 'probe', [(q, q ^ 1) for q in range(probe_count)])  0.99 us
    pallas_call x1, Pallas kernels, body(): pl.pallas_call(functools.partial(last_kernel, probe_count=probe_count), i...  0.73 us
  transfers between devices with their start and end apart: 1, of which 1 were waited for; matrix products, arithmetic and copies ran while one was open for 0% of the time, Pallas kernels for 0%

profile of v4, /device:TPU:0, one launch (start us, length us, event | category | flops | bytes accessed | tf_op | source)
XLA Modules:
  0.0 19.9 jit_solution(7624347162919859865)
XLA Ops:
  0.6 1.9 %first.1 = bf16[32,16,128]{2,1,0:T(8,128)(2,1)S(1)} custom-call(bf16[256,2048]{1,0:T(8,128)(2,1)} %dosage.1, f32[1,2048]{1,0:T(1,128)} %bitcast.2, bf16[8,256]{1,0:T(8,128)(2,1)} %probes.1), custom_call_target="tpu_custom_call" | custom-call | tf_op jit(solution)/shard_map/first/pallas_call | solution.py:144
  2.5 15.3 %all_to_all.5.got = bf16[32,16,128]{2,1,0:T(8,128)(2,1)S(1)} all-to-all(bf16[32,16,128]{2,1,0:T(8,128)(2,1)S(1)} %first.1), channel_id=1, replica_groups=mesh['snp'=8,'probe'=4] {'snp','probe'}, dimensions={0} | all-to-all | bytes 262144 | tf_op jit(solution)/shard_map/all_to_all | solution.py:160
  17.9 0.0 copy-start
  17.9 0.3 %collective-permute-start = (f32[56,128]{1,0:T(8,128)S(1)}, f32[56,128]{1,0:T(8,128)S(1)}, u32[]{:S(2)}, u32[]{:S(2)}) collective-permute-start(f32[56,128]{1,0:T(8,128)S(1)} %get-tuple-element.8.share), channel_id=1, source_target_pairs={{0,1},{1,0},{2,3},{3,2},{4,5},{5,4},{6,7},{7,6},{8,9},{9,8},{10,11... | collective-permute-start | bytes 86024 | tf_op jit(solution)/shard_map/ppermute | solution.py:173
  18.2 1.0 %collective-permute-done.other = f32[56,128]{1,0:T(8,128)S(1)} collective-permute-done((f32[56,128]{1,0:T(8,128)S(1)}, f32[56,128]{1,0:T(8,128)S(1)}, u32[]{:S(2)}, u32[]{:S(2)}) %collective-permute-start) | collective-permute-done | bytes 28704 | tf_op jit(solution)/shard_map/ppermute | solution.py:173
  19.1 0.0 copy-done
  19.2 0.7 %last.1 = (f32[8,32]{1,0:T(8,128)}, f32[2,8]{1,0:T(2,128)}, f32[1,2]{1,0:T(1,128)}) custom-call(f32[56,128]{1,0:T(8,128)S(1)} %get-tuple-element.8.share, f32[56,128]{1,0:T(8,128)S(1)} %collective-permute-done.other, f32[8,128]{1,0:T(8,128)S(1)} %get-tuple-element.9.own, bf16[8,256]{1,0:T(8,128)(2,1)S(1)} %copy-done), custom_call_target="tpu_custom_call" | custom-call | tf_op jit(solution)/shard_map/last/pallas_call | solution.py:174
  (1 shorter events, 0.0 us)
Async XLA Ops:
  17.9 1.3 %copy-start = (bf16[8,256]{1,0:T(8,128)(2,1)S(1)}, bf16[8,256]{1,0:T(8,128)(2,1)}, u32[]{:S(2)}) copy-start(bf16[8,256]{1,0:T(8,128)(2,1)} %probes.1) | copy-start | bytes 12292
  17.9 1.3 %collective-permute-start = (f32[56,128]{1,0:T(8,128)S(1)}, f32[56,128]{1,0:T(8,128)S(1)}, u32[]{:S(2)}, u32[]{:S(2)}) collective-permute-start(f32[56,128]{1,0:T(8,128)S(1)} %get-tuple-element.8.share), channel_id=1, source_target_pairs={{0,1},{1,0},{2,3},{3,2},{4,5},{5,4},{6,7},{7,6},{8,9},{9,8},{10,11... | collective-permute-start | bytes 86024 | tf_op jit(solution)/shard_map/ppermute | solution.py:173

commit v5 on v4

--- a/solution.py
+++ b/solution.py
@@ -7,7 +7,7 @@
 from jax.experimental.pallas import tpu as pltpu
 from jax.sharding import PartitionSpec as P
 
-BOTH = ("snp", "probe")
+BOTH = ("probe", "snp")
 ACROSS = (((1,), (1,)), ((), ()))
 CHUNKS = 2
 
@@ -64,7 +64,7 @@
     for i in range(snp_count):
         block = jnp.concatenate([signed, kinship[i * part : (i + 1) * part]], axis=0)
         for q in range(probe_count):
-            send[i * probe_count + q] = block[:, (q % 2) * half : (q % 2 + 1) * half]
+            send[q * snp_count + i] = block[:, (q % 2) * half : (q % 2 + 1) * half]
 
 
 def sum_kernel(got, share, own, sums, *, snp_count, probe_count, rows):
@@ -75,9 +75,9 @@
     first = jnp.zeros((rows, got.shape[2]), jnp.float32)
     second = first
     for q in range(probe_count):
-        summed = got[q].astype(jnp.float32)
+        summed = got[q * snp_count].astype(jnp.float32)
         for j in range(1, snp_count):
-            summed = summed + got[j * probe_count + q].astype(jnp.float32)
+            summed = summed + got[q * snp_count + j].astype(jnp.float32)
         signed = summed[:rows]
         sums[q] = signed
         share[q * part : (q + 1) * part] = summed[rows:]

time: 20.1 us -> 19.7 us (0.980)
  blocking collectives: 15.3 us -> 14.9 us
    all_to_all x1, blocking collectives: 15.3 us -> 14.9 us  [body(): got = lax.all_to_all(send, BOTH, 0, 0, tiled=True)]
where the time goes in v5:
time: 19.7 us; the launch traced here: 19.5 us
  blocking collectives  14.9 us (76%)
  Pallas kernels  2.64 us (13%)
  waiting for transfers between devices  1.09 us (6%)
  between operations  0.64 us (3%)
    all_to_all x1, blocking collectives, body(): got = lax.all_to_all(send, BOTH, 0, 0, tiled=True)  14.9 us
    pallas_call x1, Pallas kernels, body(): pl.pallas_call(functools.partial(first_kernel, snp_count=snp_count, probe...  1.88 us
    ppermute x1, waiting for transfers between devices, body(): lax.ppermute(share, 'probe', [(q, q ^ 1) for q in range(probe_count)])  1.09 us
    pallas_call x1, Pallas kernels, body(): pl.pallas_call(functools.partial(last_kernel, probe_count=probe_count), i...  0.73 us
  transfers between devices with their start and end apart: 1, of which 1 were waited for; matrix products, arithmetic and copies ran while one was open for 0% of the time, Pallas kernels for 0%

profile of v5, /device:TPU:0, one launch (start us, length us, event | category | flops | bytes accessed | tf_op | source)
XLA Modules:
  0.0 19.5 jit_solution(10082781144878660969)
XLA Ops:
  0.6 1.9 %first.1 = bf16[32,16,128]{2,1,0:T(8,128)(2,1)S(1)} custom-call(bf16[256,2048]{1,0:T(8,128)(2,1)} %dosage.1, f32[1,2048]{1,0:T(1,128)} %bitcast.2, bf16[8,256]{1,0:T(8,128)(2,1)} %probes.1), custom_call_target="tpu_custom_call" | custom-call | tf_op jit(solution)/shard_map/first/pallas_call | solution.py:144
  2.5 14.9 %all_to_all.5.got = bf16[32,16,128]{2,1,0:T(8,128)(2,1)S(1)} all-to-all(bf16[32,16,128]{2,1,0:T(8,128)(2,1)S(1)} %first.1), channel_id=1, replica_groups=mesh['snp'=8,'probe'=4] {'probe','snp'}, dimensions={0} | all-to-all | bytes 262144 | tf_op jit(solution)/shard_map/all_to_all | solution.py:160
  17.5 0.0 copy-start
  17.5 0.2 collective-permute-start
  17.7 1.1 %collective-permute-done.other = f32[56,128]{1,0:T(8,128)S(1)} collective-permute-done((f32[56,128]{1,0:T(8,128)S(1)}, f32[56,128]{1,0:T(8,128)S(1)}, u32[]{:S(2)}, u32[]{:S(2)}) %collective-permute-start) | collective-permute-done | bytes 28704 | tf_op jit(solution)/shard_map/ppermute | solution.py:173
  18.8 0.0 copy-done
  18.8 0.7 %last.1 = (f32[8,32]{1,0:T(8,128)}, f32[2,8]{1,0:T(2,128)}, f32[1,2]{1,0:T(1,128)}) custom-call(f32[56,128]{1,0:T(8,128)S(1)} %get-tuple-element.8.share, f32[56,128]{1,0:T(8,128)S(1)} %collective-permute-done.other, f32[8,128]{1,0:T(8,128)S(1)} %get-tuple-element.9.own, bf16[8,256]{1,0:T(8,128)(2,1)S(1)} %copy-done), custom_call_target="tpu_custom_call" | custom-call | tf_op jit(solution)/shard_map/last/pallas_call | solution.py:174
  (1 shorter events, 0.0 us)
Async XLA Ops:
  17.5 1.3 %copy-start = (bf16[8,256]{1,0:T(8,128)(2,1)S(1)}, bf16[8,256]{1,0:T(8,128)(2,1)}, u32[]{:S(2)}) copy-start(bf16[8,256]{1,0:T(8,128)(2,1)} %probes.1) | copy-start | bytes 12292
  17.5 1.3 %collective-permute-start = (f32[56,128]{1,0:T(8,128)S(1)}, f32[56,128]{1,0:T(8,128)S(1)}, u32[]{:S(2)}, u32[]{:S(2)}) collective-permute-start(f32[56,128]{1,0:T(8,128)S(1)} %get-tuple-element.8.share), channel_id=1, source_target_pairs={{0,1},{1,0},{2,3},{3,2},{4,5},{5,4},{6,7},{7,6},{8,9},{9,8},{10,11... | collective-permute-start | bytes 86024 | tf_op jit(solution)/shard_map/ppermute | solution.py:173

commit v6 on v5

--- a/solution.py
+++ b/solution.py
@@ -10,6 +10,42 @@
 BOTH = ("probe", "snp")
 ACROSS = (((1,), (1,)), ((), ()))
 CHUNKS = 2
+TILE = 256
+
+
+def tiled_products(left, weight, mean, square, copies, stage):
+    height = left.shape[0]
+    acc = [pltpu.ACC(q)((height, TILE), jnp.float32) for q in (0, 1) for _ in range(3)]
+    width = stage.shape[2]
+
+    def run(raw00, raw01, sum0, raw10, raw11, sum1):
+        raws = ((raw00, raw01), (raw10, raw11))
+        sums = (sum0, sum1)
+        shift = jnp.zeros((height, TILE), jnp.float32)
+        for c, copy in enumerate(copies):
+            copy.wait()
+
+            def tile(k, q):
+                return slice((2 * k + q) * TILE, (2 * k + q + 1) * TILE)
+
+            for k in (0, 1):
+                for q in (0, 1):
+                    pltpu.matmul_push_rhs(stage[c, :, tile(k, q)], k, q)
+            for k in (0, 1):
+                for q in (0, 1):
+                    pltpu.matmul_acc_lhs(raws[q][k], left, load_staged_rhs=k)
+                    pltpu.matmul_push_rhs(stage[c, :, tile(k, q)], k, q, transpose=True)
+            for k in (0, 1):
+                for q in (0, 1):
+                    at = slice(c * width + tile(k, q).start, c * width + tile(k, q).stop)
+                    m = mean[:, at]
+                    raw = pltpu.matmul_pop(raws[q][k])
+                    scaled = ((raw - weight * m) * square[:, at]).astype(jnp.bfloat16)
+                    pltpu.matmul_acc_lhs(sums[q], scaled, load_staged_rhs=k)
+                    shift = shift + scaled.astype(jnp.float32) * m
+        return pltpu.matmul_pop(sum0) + pltpu.matmul_pop(sum1), shift
+
+    return pl.run_scoped(run, *acc)
 
 
 def first_kernel(
@@ -38,25 +74,30 @@
     for copy in small:
         copy.wait()
     signs = probes[...]
-    left = jnp.concatenate([signs, pick], axis=0)
+    blank = jnp.zeros((-(rows + pick.shape[0]) % 16, samples), jnp.bfloat16)
+    left = jnp.concatenate([signs, pick, blank], axis=0)
     weight = jnp.sum(left.astype(jnp.float32), axis=1, keepdims=True)
     mean = 2.0 * freq[...]
     square = 1.0 / (mean * (1.0 - 0.5 * mean))
-    total = jnp.zeros((left.shape[0], samples), jnp.float32)
-    shift = jnp.zeros((left.shape[0], step), jnp.float32)
-    for c in range(CHUNKS):
-        m = mean[:, c * step : (c + 1) * step]
-        copies[c].wait()
-        raw = jnp.dot(left, stage[c], preferred_element_type=jnp.float32)
-        if c:
-            total = total + lax.dot_general(
-                scaled, stage[c - 1], ACROSS, preferred_element_type=jnp.float32
-            )
-        scaled = ((raw - weight * m) * square[:, c * step : (c + 1) * step]).astype(jnp.bfloat16)
-        shift = shift + scaled.astype(jnp.float32) * m
-    total = total + lax.dot_general(
-        scaled, stage[CHUNKS - 1], ACROSS, preferred_element_type=jnp.float32
-    )
+    if samples == TILE and step == 4 * TILE:
+        total, shift = tiled_products(left, weight, mean, square, copies, stage)
+    else:
+        total = jnp.zeros((left.shape[0], samples), jnp.float32)
+        shift = jnp.zeros((left.shape[0], step), jnp.float32)
+        for c in range(CHUNKS):
+            m = mean[:, c * step : (c + 1) * step]
+            copies[c].wait()
+            raw = jnp.dot(left, stage[c], preferred_element_type=jnp.float32)
+            if c:
+                total = total + lax.dot_general(
+                    scaled, stage[c - 1], ACROSS, preferred_element_type=jnp.float32
+                )
+            scaled = raw - weight * m
+            scaled = (scaled * square[:, c * step : (c + 1) * step]).astype(jnp.bfloat16)
+            shift = shift + scaled.astype(jnp.float32) * m
+        total = total + lax.dot_general(
+            scaled, stage[CHUNKS - 1], ACROSS, preferred_element_type=jnp.float32
+        )
     total = (total - jnp.sum(shift, axis=1, keepdims=True)) * (1.0 / columns)
     signed = (signs.astype(jnp.float32) * total[:rows]).astype(jnp.bfloat16)
     kinship = total[rows:].astype(jnp.bfloat16)

time: 19.7 us -> 19.6 us (level)
  no operation moved by 1% of the time
where the time goes in v6:
time: 19.6 us; the launch traced here: 19.4 us
  blocking collectives  14.9 us (76%)
  Pallas kernels  2.52 us (13%)
  waiting for transfers between devices  1.09 us (6%)
  between operations  0.64 us (3%)
    all_to_all x1, blocking collectives, body(): got = lax.all_to_all(send, BOTH, 0, 0, tiled=True)  14.9 us
    pallas_call x1, Pallas kernels, body(): pl.pallas_call(functools.partial(first_kernel, snp_count=snp_count, probe...  1.77 us
    ppermute x1, waiting for transfers between devices, body(): lax.ppermute(share, 'probe', [(q, q ^ 1) for q in range(probe_count)])  1.09 us
    pallas_call x1, Pallas kernels, body(): pl.pallas_call(functools.partial(last_kernel, probe_count=probe_count), i...  0.73 us
  transfers between devices with their start and end apart: 1, of which 1 were waited for; matrix products, arithmetic and copies ran while one was open for 0% of the time, Pallas kernels for 0%

profile of v6, /device:TPU:0, one launch (start us, length us, event | category | flops | bytes accessed | tf_op | source)
XLA Modules:
  0.0 19.4 jit_solution(223542167355447240)
XLA Ops:
  0.6 1.8 %first.1 = bf16[32,16,128]{2,1,0:T(8,128)(2,1)S(1)} custom-call(bf16[256,2048]{1,0:T(8,128)(2,1)} %dosage.1, f32[1,2048]{1,0:T(1,128)} %bitcast.2, bf16[8,256]{1,0:T(8,128)(2,1)} %probes.1), custom_call_target="tpu_custom_call" | custom-call | tf_op jit(solution)/shard_map/first/pallas_call | solution.py:185
  2.4 14.9 %all_to_all.5.got = bf16[32,16,128]{2,1,0:T(8,128)(2,1)S(1)} all-to-all(bf16[32,16,128]{2,1,0:T(8,128)(2,1)S(1)} %first.1), channel_id=1, replica_groups=mesh['snp'=8,'probe'=4] {'probe','snp'}, dimensions={0} | all-to-all | bytes 262144 | tf_op jit(solution)/shard_map/all_to_all | solution.py:201
  17.3 0.0 copy-start
  17.4 0.2 collective-permute-start
  17.6 1.1 %collective-permute-done.other = f32[56,128]{1,0:T(8,128)S(1)} collective-permute-done((f32[56,128]{1,0:T(8,128)S(1)}, f32[56,128]{1,0:T(8,128)S(1)}, u32[]{:S(2)}, u32[]{:S(2)}) %collective-permute-start) | collective-permute-done | bytes 28704 | tf_op jit(solution)/shard_map/ppermute | solution.py:214
  18.6 0.0 copy-done
  18.6 0.7 %last.1 = (f32[8,32]{1,0:T(8,128)}, f32[2,8]{1,0:T(2,128)}, f32[1,2]{1,0:T(1,128)}) custom-call(f32[56,128]{1,0:T(8,128)S(1)} %get-tuple-element.8.share, f32[56,128]{1,0:T(8,128)S(1)} %collective-permute-done.other, f32[8,128]{1,0:T(8,128)S(1)} %get-tuple-element.9.own, bf16[8,256]{1,0:T(8,128)(2,1)S(1)} %copy-done), custom_call_target="tpu_custom_call" | custom-call | tf_op jit(solution)/shard_map/last/pallas_call | solution.py:215
  (1 shorter events, 0.0 us)
Async XLA Ops:
  17.3 1.3 %copy-start = (bf16[8,256]{1,0:T(8,128)(2,1)S(1)}, bf16[8,256]{1,0:T(8,128)(2,1)}, u32[]{:S(2)}) copy-start(bf16[8,256]{1,0:T(8,128)(2,1)} %probes.1) | copy-start | bytes 12292
  17.4 1.3 %collective-permute-start = (f32[56,128]{1,0:T(8,128)S(1)}, f32[56,128]{1,0:T(8,128)S(1)}, u32[]{:S(2)}, u32[]{:S(2)}) collective-permute-start(f32[56,128]{1,0:T(8,128)S(1)} %get-tuple-element.8.share), channel_id=1, source_target_pairs={{0,1},{1,0},{2,3},{3,2},{4,5},{5,4},{6,7},{7,6},{8,9},{9,8},{10,11... | collective-permute-start | bytes 86024 | tf_op jit(solution)/shard_map/ppermute | solution.py:214

commit v7 on v6

--- a/solution.py
+++ b/solution.py
@@ -22,6 +22,8 @@
         raws = ((raw00, raw01), (raw10, raw11))
         sums = (sum0, sum1)
         shift = jnp.zeros((height, TILE), jnp.float32)
+        for ref in (*raws[0], *raws[1], *sums):
+            pltpu.matmul_pop(ref)
         for c, copy in enumerate(copies):
             copy.wait()
 

time: 19.6 us -> 19.6 us (level)
  no operation moved by 1% of the time
where the time goes in v7:
time: 19.6 us; the launch traced here: 19.4 us
  blocking collectives  14.9 us (76%)
  Pallas kernels  2.52 us (13%)
  waiting for transfers between devices  1.09 us (6%)
  between operations  0.64 us (3%)
    all_to_all x1, blocking collectives, body(): got = lax.all_to_all(send, BOTH, 0, 0, tiled=True)  14.9 us
    pallas_call x1, Pallas kernels, body(): pl.pallas_call(functools.partial(first_kernel, snp_count=snp_count, probe...  1.77 us
    ppermute x1, waiting for transfers between devices, body(): lax.ppermute(share, 'probe', [(q, q ^ 1) for q in range(probe_count)])  1.09 us
    pallas_call x1, Pallas kernels, body(): pl.pallas_call(functools.partial(last_kernel, probe_count=probe_count), i...  0.73 us
  transfers between devices with their start and end apart: 1, of which 1 were waited for; matrix products, arithmetic and copies ran while one was open for 0% of the time, Pallas kernels for 0%

profile of v7, /device:TPU:0, one launch (start us, length us, event | category | flops | bytes accessed | tf_op | source)
XLA Modules:
  0.0 19.4 jit_solution(6340780100293797580)
XLA Ops:
  0.6 1.8 %first.1 = bf16[32,16,128]{2,1,0:T(8,128)(2,1)S(1)} custom-call(bf16[256,2048]{1,0:T(8,128)(2,1)} %dosage.1, f32[1,2048]{1,0:T(1,128)} %bitcast.2, bf16[8,256]{1,0:T(8,128)(2,1)} %probes.1), custom_call_target="tpu_custom_call" | custom-call | tf_op jit(solution)/shard_map/first/pallas_call | solution.py:187
  2.4 14.9 %all_to_all.5.got = bf16[32,16,128]{2,1,0:T(8,128)(2,1)S(1)} all-to-all(bf16[32,16,128]{2,1,0:T(8,128)(2,1)S(1)} %first.1), channel_id=1, replica_groups=mesh['snp'=8,'probe'=4] {'probe','snp'}, dimensions={0} | all-to-all | bytes 262144 | tf_op jit(solution)/shard_map/all_to_all | solution.py:203
  17.3 0.0 copy-start
  17.4 0.2 collective-permute-start
  17.6 1.1 %collective-permute-done.other = f32[56,128]{1,0:T(8,128)S(1)} collective-permute-done((f32[56,128]{1,0:T(8,128)S(1)}, f32[56,128]{1,0:T(8,128)S(1)}, u32[]{:S(2)}, u32[]{:S(2)}) %collective-permute-start) | collective-permute-done | bytes 28704 | tf_op jit(solution)/shard_map/ppermute | solution.py:216
  18.6 0.0 copy-done
  18.6 0.7 %last.1 = (f32[8,32]{1,0:T(8,128)}, f32[2,8]{1,0:T(2,128)}, f32[1,2]{1,0:T(1,128)}) custom-call(f32[56,128]{1,0:T(8,128)S(1)} %get-tuple-element.8.share, f32[56,128]{1,0:T(8,128)S(1)} %collective-permute-done.other, f32[8,128]{1,0:T(8,128)S(1)} %get-tuple-element.9.own, bf16[8,256]{1,0:T(8,128)(2,1)S(1)} %copy-done), custom_call_target="tpu_custom_call" | custom-call | tf_op jit(solution)/shard_map/last/pallas_call | solution.py:217
  (1 shorter events, 0.0 us)
Async XLA Ops:
  17.3 1.3 %copy-start = (bf16[8,256]{1,0:T(8,128)(2,1)S(1)}, bf16[8,256]{1,0:T(8,128)(2,1)}, u32[]{:S(2)}) copy-start(bf16[8,256]{1,0:T(8,128)(2,1)} %probes.1) | copy-start | bytes 12292
  17.4 1.3 %collective-permute-start = (f32[56,128]{1,0:T(8,128)S(1)}, f32[56,128]{1,0:T(8,128)S(1)}, u32[]{:S(2)}, u32[]{:S(2)}) collective-permute-start(f32[56,128]{1,0:T(8,128)S(1)} %get-tuple-element.8.share), channel_id=1, source_target_pairs={{0,1},{1,0},{2,3},{3,2},{4,5},{5,4},{6,7},{7,6},{8,9},{9,8},{10,11... | collective-permute-start | bytes 86024 | tf_op jit(solution)/shard_map/ppermute | solution.py:216

commit v8 on v7

--- a/solution.py
+++ b/solution.py
@@ -13,7 +13,7 @@
 TILE = 256
 
 
-def tiled_products(left, weight, mean, square, copies, stage):
+def tiled_products(left, mean, scaling, copies, stage, standard):
     height = left.shape[0]
     acc = [pltpu.ACC(q)((height, TILE), jnp.float32) for q in (0, 1) for _ in range(3)]
     width = stage.shape[2]
@@ -21,7 +21,6 @@
     def run(raw00, raw01, sum0, raw10, raw11, sum1):
         raws = ((raw00, raw01), (raw10, raw11))
         sums = (sum0, sum1)
-        shift = jnp.zeros((height, TILE), jnp.float32)
         for ref in (*raws[0], *raws[1], *sums):
             pltpu.matmul_pop(ref)
         for c, copy in enumerate(copies):
@@ -32,26 +31,27 @@
 
             for k in (0, 1):
                 for q in (0, 1):
-                    pltpu.matmul_push_rhs(stage[c, :, tile(k, q)], k, q)
+                    at = slice(c * width + tile(k, q).start, c * width + tile(k, q).stop)
+                    dosages = stage[c, :, tile(k, q)].astype(jnp.float32)
+                    standard[c, :, tile(k, q)] = (
+                        (dosages - mean[:, at]) * scaling[:, at]
+                    ).astype(jnp.bfloat16)
+                    pltpu.matmul_push_rhs(standard[c, :, tile(k, q)], k, q)
             for k in (0, 1):
                 for q in (0, 1):
                     pltpu.matmul_acc_lhs(raws[q][k], left, load_staged_rhs=k)
-                    pltpu.matmul_push_rhs(stage[c, :, tile(k, q)], k, q, transpose=True)
+                    pltpu.matmul_push_rhs(standard[c, :, tile(k, q)], k, q, transpose=True)
             for k in (0, 1):
                 for q in (0, 1):
-                    at = slice(c * width + tile(k, q).start, c * width + tile(k, q).stop)
-                    m = mean[:, at]
-                    raw = pltpu.matmul_pop(raws[q][k])
-                    scaled = ((raw - weight * m) * square[:, at]).astype(jnp.bfloat16)
-                    pltpu.matmul_acc_lhs(sums[q], scaled, load_staged_rhs=k)
-                    shift = shift + scaled.astype(jnp.float32) * m
-        return pltpu.matmul_pop(sum0) + pltpu.matmul_pop(sum1), shift
+                    projected = pltpu.matmul_pop(raws[q][k]).astype(jnp.bfloat16)
+                    pltpu.matmul_acc_lhs(sums[q], projected, load_staged_rhs=k)
+        return pltpu.matmul_pop(sum0) + pltpu.matmul_pop(sum1)
 
     return pl.run_scoped(run, *acc)
 
 
 def first_kernel(
-    dosage, freq_hbm, probes_hbm, send, stage, freq, probes, sems, *, snp_count, probe_count, columns
+    dosage, freq_hbm, probes_hbm, send, stage, standard, freq, probes, sems, *, snp_count, probe_count, columns
 ):
     samples, width = dosage.shape
     rows = probes.shape[0]
@@ -78,29 +78,26 @@
     signs = probes[...]
     blank = jnp.zeros((-(rows + pick.shape[0]) % 16, samples), jnp.bfloat16)
     left = jnp.concatenate([signs, pick, blank], axis=0)
-    weight = jnp.sum(left.astype(jnp.float32), axis=1, keepdims=True)
     mean = 2.0 * freq[...]
-    square = 1.0 / (mean * (1.0 - 0.5 * mean))
+    scaling = lax.rsqrt(mean * (1.0 - 0.5 * mean))
     if samples == TILE and step == 4 * TILE:
-        total, shift = tiled_products(left, weight, mean, square, copies, stage)
+        total = tiled_products(left, mean, scaling, copies, stage, standard)
     else:
         total = jnp.zeros((left.shape[0], samples), jnp.float32)
-        shift = jnp.zeros((left.shape[0], step), jnp.float32)
         for c in range(CHUNKS):
-            m = mean[:, c * step : (c + 1) * step]
+            at = slice(c * step, (c + 1) * step)
             copies[c].wait()
-            raw = jnp.dot(left, stage[c], preferred_element_type=jnp.float32)
-            if c:
-                total = total + lax.dot_general(
-                    scaled, stage[c - 1], ACROSS, preferred_element_type=jnp.float32
-                )
-            scaled = raw - weight * m
-            scaled = (scaled * square[:, c * step : (c + 1) * step]).astype(jnp.bfloat16)
-            shift = shift + scaled.astype(jnp.float32) * m
-        total = total + lax.dot_general(
-            scaled, stage[CHUNKS - 1], ACROSS, preferred_element_type=jnp.float32
-        )
-    total = (total - jnp.sum(shift, axis=1, keepdims=True)) * (1.0 / columns)
+            standard[c] = ((stage[c].astype(jnp.float32) - mean[:, at]) * scaling[:, at]).astype(
+                jnp.bfloat16
+            )
+            projected = jnp.dot(left, standard[c], preferred_element_type=jnp.float32)
+            total = total + lax.dot_general(
+                projected.astype(jnp.bfloat16),
+                standard[c],
+                ACROSS,
+                preferred_element_type=jnp.float32,
+            )
+    total = total * (1.0 / columns)
     signed = (signs.astype(jnp.float32) * total[:rows]).astype(jnp.bfloat16)
     kinship = total[rows:].astype(jnp.bfloat16)
     half = samples // 2
@@ -193,6 +190,7 @@
         out_shape=jax.ShapeDtypeStruct((devices, rows + part, half), jnp.bfloat16),
         scratch_shapes=[
             pltpu.VMEM((CHUNKS, samples, width // CHUNKS), jnp.bfloat16),
+            pltpu.VMEM((CHUNKS, samples, width // CHUNKS), jnp.bfloat16),
             pltpu.VMEM((1, width), jnp.float32),
             pltpu.VMEM((rows, samples), jnp.bfloat16),
             pltpu.SemaphoreType.DMA((CHUNKS + 2,)),

time: 19.6 us -> 19.7 us (level)
  no operation moved by 1% of the time
where the time goes in v8:
time: 19.7 us; the launch traced here: 19.5 us
  blocking collectives  14.9 us (76%)
  Pallas kernels  2.64 us (13%)
  waiting for transfers between devices  1.09 us (6%)
  between operations  0.64 us (3%)
    all_to_all x1, blocking collectives, body(): got = lax.all_to_all(send, BOTH, 0, 0, tiled=True)  14.9 us
    pallas_call x1, Pallas kernels, body(): pl.pallas_call(functools.partial(first_kernel, snp_count=snp_count, probe...  1.88 us
    ppermute x1, waiting for transfers between devices, body(): lax.ppermute(share, 'probe', [(q, q ^ 1) for q in range(probe_count)])  1.09 us
    pallas_call x1, Pallas kernels, body(): pl.pallas_call(functools.partial(last_kernel, probe_count=probe_count), i...  0.73 us
  transfers between devices with their start and end apart: 1, of which 1 were waited for; matrix products, arithmetic and copies ran while one was open for 0% of the time, Pallas kernels for 0%

profile of v8, /device:TPU:0, one launch (start us, length us, event | category | flops | bytes accessed | tf_op | source)
XLA Modules:
  0.0 19.5 jit_solution(4700322829267510020)
XLA Ops:
  0.6 1.9 %first.1 = bf16[32,16,128]{2,1,0:T(8,128)(2,1)S(1)} custom-call(bf16[256,2048]{1,0:T(8,128)(2,1)} %dosage.1, f32[1,2048]{1,0:T(1,128)} %bitcast.2, bf16[8,256]{1,0:T(8,128)(2,1)} %probes.1), custom_call_target="tpu_custom_call" | custom-call | tf_op jit(solution)/shard_map/first/pallas_call | solution.py:184
  2.5 14.9 %all_to_all.5.got = bf16[32,16,128]{2,1,0:T(8,128)(2,1)S(1)} all-to-all(bf16[32,16,128]{2,1,0:T(8,128)(2,1)S(1)} %first.1), channel_id=1, replica_groups=mesh['snp'=8,'probe'=4] {'probe','snp'}, dimensions={0} | all-to-all | bytes 262144 | tf_op jit(solution)/shard_map/all_to_all | solution.py:201
  17.5 0.0 copy-start
  17.5 0.2 collective-permute-start
  17.7 1.1 %collective-permute-done.other = f32[56,128]{1,0:T(8,128)S(1)} collective-permute-done((f32[56,128]{1,0:T(8,128)S(1)}, f32[56,128]{1,0:T(8,128)S(1)}, u32[]{:S(2)}, u32[]{:S(2)}) %collective-permute-start) | collective-permute-done | bytes 28704 | tf_op jit(solution)/shard_map/ppermute | solution.py:214
  18.8 0.0 copy-done
  18.8 0.7 %last.1 = (f32[8,32]{1,0:T(8,128)}, f32[2,8]{1,0:T(2,128)}, f32[1,2]{1,0:T(1,128)}) custom-call(f32[56,128]{1,0:T(8,128)S(1)} %get-tuple-element.8.share, f32[56,128]{1,0:T(8,128)S(1)} %collective-permute-done.other, f32[8,128]{1,0:T(8,128)S(1)} %get-tuple-element.9.own, bf16[8,256]{1,0:T(8,128)(2,1)S(1)} %copy-done), custom_call_target="tpu_custom_call" | custom-call | tf_op jit(solution)/shard_map/last/pallas_call | solution.py:215
  (1 shorter events, 0.0 us)
Async XLA Ops:
  17.5 1.3 %copy-start = (bf16[8,256]{1,0:T(8,128)(2,1)S(1)}, bf16[8,256]{1,0:T(8,128)(2,1)}, u32[]{:S(2)}) copy-start(bf16[8,256]{1,0:T(8,128)(2,1)} %probes.1) | copy-start | bytes 12292
  17.5 1.3 %collective-permute-start = (f32[56,128]{1,0:T(8,128)S(1)}, f32[56,128]{1,0:T(8,128)S(1)}, u32[]{:S(2)}, u32[]{:S(2)}) collective-permute-start(f32[56,128]{1,0:T(8,128)S(1)} %get-tuple-element.8.share), channel_id=1, source_target_pairs={{0,1},{1,0},{2,3},{3,2},{4,5},{5,4},{6,7},{7,6},{8,9},{9,8},{10,11... | collective-permute-start | bytes 86024 | tf_op jit(solution)/shard_map/ppermute | solution.py:214

commit v9 on v8

--- a/solution.py
+++ b/solution.py
@@ -98,17 +98,19 @@
                 preferred_element_type=jnp.float32,
             )
     total = total * (1.0 / columns)
-    signed = (signs.astype(jnp.float32) * total[:rows]).astype(jnp.bfloat16)
+    exact = signs.astype(jnp.float32) * total[:rows]
+    signed = exact.astype(jnp.bfloat16)
+    rest = (exact - signed.astype(jnp.float32)).astype(jnp.bfloat16)
     kinship = total[rows:].astype(jnp.bfloat16)
     half = samples // 2
     for i in range(snp_count):
-        block = jnp.concatenate([signed, kinship[i * part : (i + 1) * part]], axis=0)
+        block = jnp.concatenate([signed, rest, kinship[i * part : (i + 1) * part]], axis=0)
         for q in range(probe_count):
             send[q * snp_count + i] = block[:, (q % 2) * half : (q % 2 + 1) * half]
 
 
 def sum_kernel(got, share, own, sums, *, snp_count, probe_count, rows):
-    part = got.shape[1] - rows
+    part = got.shape[1] - 2 * rows
     owned = part * probe_count
     group = lax.axis_index("probe")
     partner = group + 1 - 2 * (group % 2)
@@ -118,9 +120,9 @@
         summed = got[q * snp_count].astype(jnp.float32)
         for j in range(1, snp_count):
             summed = summed + got[q * snp_count + j].astype(jnp.float32)
-        signed = summed[:rows]
+        signed = summed[:rows] + summed[rows : 2 * rows]
         sums[q] = signed
-        share[q * part : (q + 1) * part] = summed[rows:]
+        share[q * part : (q + 1) * part] = summed[2 * rows :]
         first = first + signed
         second = second + signed.astype(jnp.bfloat16).astype(jnp.float32) * signed
     share[owned : owned + rows] = first
@@ -187,7 +189,7 @@
         ),
         in_specs=[hbm, hbm, hbm],
         out_specs=vmem,
-        out_shape=jax.ShapeDtypeStruct((devices, rows + part, half), jnp.bfloat16),
+        out_shape=jax.ShapeDtypeStruct((devices, 2 * rows + part, half), jnp.bfloat16),
         scratch_shapes=[
             pltpu.VMEM((CHUNKS, samples, width // CHUNKS), jnp.bfloat16),
             pltpu.VMEM((CHUNKS, samples, width // CHUNKS), jnp.bfloat16),

time: 19.7 us -> 20.3 us (1.030)
  blocking collectives: 14.9 us -> 15.4 us
  starting transfers between devices: 0.18 us -> 0.51 us
  waiting for transfers between devices: 1.09 us -> 0.85 us
    all_to_all x1, blocking collectives: 14.9 us -> 15.4 us  [body(): got = lax.all_to_all(send, BOTH, 0, 0, tiled=True)]
    ppermute x1, starting transfers between devices: 0.18 us -> 0.51 us  [body(): lax.ppermute(share, 'probe', [(q, q ^ 1) for q in range(probe_count)])]
    ppermute x1, waiting for transfers between devices: 1.09 us -> 0.85 us  [body(): lax.ppermute(share, 'probe', [(q, q ^ 1) for q in range(probe_count)])]
where the time goes in v9:
time: 20.3 us; the launch traced here: 20 us
  blocking collectives  15.4 us (76%)
  Pallas kernels  2.65 us (13%)
  waiting for transfers between devices  0.85 us (4%)
  between operations  0.64 us (3%)
  starting transfers between devices  0.51 us (3%)
    all_to_all x1, blocking collectives, body(): got = lax.all_to_all(send, BOTH, 0, 0, tiled=True)  15.4 us
    pallas_call x1, Pallas kernels, body(): pl.pallas_call(functools.partial(first_kernel, snp_count=snp_count, probe...  1.89 us
    ppermute x1, waiting for transfers between devices, body(): lax.ppermute(share, 'probe', [(q, q ^ 1) for q in range(probe_count)])  0.85 us
    pallas_call x1, Pallas kernels, body(): pl.pallas_call(functools.partial(last_kernel, probe_count=probe_count), i...  0.73 us
    ppermute x1, starting transfers between devices, body(): lax.ppermute(share, 'probe', [(q, q ^ 1) for q in range(probe_count)])  0.51 us
  transfers between devices with their start and end apart: 1, of which 1 were waited for; matrix products, arithmetic and copies ran while one was open for 0% of the time, Pallas kernels for 0%

profile of v9, /device:TPU:0, one launch (start us, length us, event | category | flops | bytes accessed | tf_op | source)
XLA Modules:
  0.0 20.0 jit_solution(2662240392562781520)
XLA Ops:
  0.6 1.9 %first.1 = bf16[32,24,128]{2,1,0:T(8,128)(2,1)S(1)} custom-call(bf16[256,2048]{1,0:T(8,128)(2,1)} %dosage.1, f32[1,2048]{1,0:T(1,128)} %bitcast.2, bf16[8,256]{1,0:T(8,128)(2,1)} %probes.1), custom_call_target="tpu_custom_call" | custom-call | tf_op jit(solution)/shard_map/first/pallas_call | solution.py:186
  2.5 15.4 %all_to_all.5.got = bf16[32,24,128]{2,1,0:T(8,128)(2,1)S(1)} all-to-all(bf16[32,24,128]{2,1,0:T(8,128)(2,1)S(1)} %first.1), channel_id=1, replica_groups=mesh['snp'=8,'probe'=4] {'probe','snp'}, dimensions={0} | all-to-all | bytes 393216 | tf_op jit(solution)/shard_map/all_to_all | solution.py:203
  17.9 0.0 copy-start
  17.9 0.5 %collective-permute-start = (f32[56,128]{1,0:T(8,128)S(1)}, f32[56,128]{1,0:T(8,128)S(1)}, u32[]{:S(2)}, u32[]{:S(2)}) collective-permute-start(f32[56,128]{1,0:T(8,128)S(1)} %get-tuple-element.8.share), channel_id=1, source_target_pairs={{0,1},{1,0},{2,3},{3,2},{4,5},{5,4},{6,7},{7,6},{8,9},{9,8},{10,11... | collective-permute-start | bytes 86024 | tf_op jit(solution)/shard_map/ppermute | solution.py:216
  18.4 0.9 %collective-permute-done.other = f32[56,128]{1,0:T(8,128)S(1)} collective-permute-done((f32[56,128]{1,0:T(8,128)S(1)}, f32[56,128]{1,0:T(8,128)S(1)}, u32[]{:S(2)}, u32[]{:S(2)}) %collective-permute-start) | collective-permute-done | bytes 28704 | tf_op jit(solution)/shard_map/ppermute | solution.py:216
  19.3 0.0 copy-done
  19.3 0.7 %last.1 = (f32[8,32]{1,0:T(8,128)}, f32[2,8]{1,0:T(2,128)}, f32[1,2]{1,0:T(1,128)}) custom-call(f32[56,128]{1,0:T(8,128)S(1)} %get-tuple-element.8.share, f32[56,128]{1,0:T(8,128)S(1)} %collective-permute-done.other, f32[8,128]{1,0:T(8,128)S(1)} %get-tuple-element.9.own, bf16[8,256]{1,0:T(8,128)(2,1)S(1)} %copy-done), custom_call_target="tpu_custom_call" | custom-call | tf_op jit(solution)/shard_map/last/pallas_call | solution.py:217
  (1 shorter events, 0.0 us)
Async XLA Ops:
  17.9 1.4 %copy-start = (bf16[8,256]{1,0:T(8,128)(2,1)S(1)}, bf16[8,256]{1,0:T(8,128)(2,1)}, u32[]{:S(2)}) copy-start(bf16[8,256]{1,0:T(8,128)(2,1)} %probes.1) | copy-start | bytes 12292
  17.9 1.4 %collective-permute-start = (f32[56,128]{1,0:T(8,128)S(1)}, f32[56,128]{1,0:T(8,128)S(1)}, u32[]{:S(2)}, u32[]{:S(2)}) collective-permute-start(f32[56,128]{1,0:T(8,128)S(1)} %get-tuple-element.8.share), channel_id=1, source_target_pairs={{0,1},{1,0},{2,3},{3,2},{4,5},{5,4},{6,7},{7,6},{8,9},{9,8},{10,11... | collective-permute-start | bytes 86024 | tf_op jit(solution)/shard_map/ppermute | solution.py:216

commit v10 on v8

--- a/solution.py
+++ b/solution.py
@@ -129,41 +129,47 @@
     own[...] = sums[group]
 
 
-def last_kernel(share, other, own, probes, kin_twice, forms, estimates, *, probe_count):
+def half_products(signed, kinship, sign):
+    rounded = signed.astype(jnp.bfloat16).astype(jnp.float32)
+    vectors = (sign * rounded).astype(jnp.bfloat16)
+    high = kinship.astype(jnp.bfloat16)
+    low = (kinship - high.astype(jnp.float32)).astype(jnp.bfloat16)
+    twice = lax.dot_general(
+        vectors, high, ACROSS, preferred_element_type=jnp.float32
+    ) + lax.dot_general(vectors, low, ACROSS, preferred_element_type=jnp.float32)
+    return twice, rounded * signed
+
+
+def half_signs(probes, own):
+    half = probes.shape[1] // 2
+    signs = probes[...].astype(jnp.float32)
+    low_half = lax.axis_index("probe") % 2 == 0
+    return jnp.where(low_half == own, signs[:, :half], signs[:, half:])
+
+
+def near_kernel(share, own, probes, near_twice, near_second):
+    owned = near_twice.shape[1]
+    near_twice[...], near_second[...] = half_products(
+        own[...], share[:owned], half_signs(probes, True)
+    )
+
+
+def last_kernel(
+    share, other, own, near_twice, near_second, probes, kin_twice, forms, estimates, *, probe_count
+):
     rows, samples = probes.shape
-    half = samples // 2
-    owned = share.shape[0] - 3 * rows
-    low_half = lax.axis_index("probe") % 2 == 0
+    owned = near_twice.shape[1]
     scale = 1.0 / samples
     mean = scale / (rows * probe_count)
     ends = share[owned : owned + 2 * rows] + other[owned : owned + 2 * rows]
     lane = lax.broadcasted_iota(jnp.int32, (1, 2), 1)
     estimates[...] = jnp.where(lane == 0, jnp.sum(ends[:rows]), jnp.sum(ends[rows:])) * mean
-    signs = probes[...].astype(jnp.float32)
-    signs_low = signs[:, :half]
-    signs_high = signs[:, half:]
-    first = jnp.zeros((rows, half), jnp.float32)
-    second = first
-    twice = jnp.zeros((rows, owned), jnp.float32)
-    for signed, rest, sign in (
-        (own[...], share, jnp.where(low_half, signs_low, signs_high)),
-        (other[owned + 2 * rows :], other, jnp.where(low_half, signs_high, signs_low)),
-    ):
-        rounded = signed.astype(jnp.bfloat16).astype(jnp.float32)
-        first = first + signed
-        second = second + rounded * signed
-        vectors = (sign * rounded).astype(jnp.bfloat16)
-        kinship = rest[:owned]
-        high = kinship.astype(jnp.bfloat16)
-        low = (kinship - high.astype(jnp.float32)).astype(jnp.bfloat16)
-        for piece in (high, low):
-            twice = twice + lax.dot_general(
-                vectors, piece, ACROSS, preferred_element_type=jnp.float32
-            )
-    kin_twice[...] = twice
+    signed = other[owned + 2 * rows :]
+    twice, second = half_products(signed, other[:owned], half_signs(probes, False))
+    kin_twice[...] = near_twice[...] + twice
     at = lax.broadcasted_iota(jnp.int32, (rows, rows), 0)
     on = at == lax.broadcasted_iota(jnp.int32, (rows, rows), 1)
-    for k, form in enumerate((first, second)):
+    for k, form in enumerate((own[...] + signed, near_second[...] + second)):
         total = jnp.sum(form, axis=1, keepdims=True) * scale
         forms[k : k + 1] = jnp.sum(jnp.where(on, total, 0.0), axis=0, keepdims=True)
 
@@ -212,9 +218,20 @@
         name="sums",
     )(got)
     other = lax.ppermute(share, "probe", [(q, q ^ 1) for q in range(probe_count)])
+    near = pl.pallas_call(
+        near_kernel,
+        in_specs=[vmem, vmem, vmem],
+        out_specs=[vmem, vmem],
+        out_shape=[
+            jax.ShapeDtypeStruct((rows, owned), jnp.float32),
+            jax.ShapeDtypeStruct((rows, half), jnp.float32),
+        ],
+        compiler_params=params,
+        name="near",
+    )(share, own, probes)
     kin_twice, forms, estimates = pl.pallas_call(
         functools.partial(last_kernel, probe_count=probe_count),
-        in_specs=[vmem, vmem, vmem, vmem],
+        in_specs=[vmem] * 6,
         out_specs=[vmem, vmem, vmem],
         out_shape=[
             jax.ShapeDtypeStruct((rows, owned), jnp.float32),
@@ -223,7 +240,7 @@
         ],
         compiler_params=params,
         name="last",
-    )(share, other, own, probes)
+    )(share, other, own, *near, probes)
     return (kin_twice, forms, estimates.reshape(2))
 
 

time: 19.7 us -> 19.8 us (level)
  waiting for transfers between devices: 1.09 us -> 0.48 us
  local copies, waits for them, and re-layouts: 0.01 us -> 0.48 us
    ppermute x1, waiting for transfers between devices: 1.09 us -> 0.48 us  [body(): lax.ppermute(share, 'probe', [(q, q ^ 1) for q in range(probe_count)])]
    unnamed x2, local copies, waits for them, and re-layouts: 0.01 us -> 0.48 us
  transfers between devices with their start and end apart: 1 -> 1, of which waited for: 1 -> 1; matrix products, arithmetic and copies ran while one was open for 0% -> 0% of each run, Pallas kernels for 0% -> 1%
where the time goes in v10:
time: 19.8 us; the launch traced here: 19.5 us
  blocking collectives  14.9 us (75%)
  Pallas kernels  2.76 us (14%)
  between operations  0.64 us (3%)
  local copies, waits for them, and re-layouts  0.48 us (2%)
  waiting for transfers between devices  0.48 us (2%)
    all_to_all x1, blocking collectives, body(): got = lax.all_to_all(send, BOTH, 0, 0, tiled=True)  14.9 us
    pallas_call x1, Pallas kernels, body(): pl.pallas_call(functools.partial(first_kernel, snp_count=snp_count, probe...  1.88 us
    pallas_call x1, Pallas kernels, body(): pl.pallas_call(functools.partial(last_kernel, probe_count=probe_count), i...  0.72 us
    ppermute x1, waiting for transfers between devices, body(): lax.ppermute(share, 'probe', [(q, q ^ 1) for q in range(probe_count)])  0.48 us
    unnamed x2, local copies, waits for them, and re-layouts  0.48 us
  transfers between devices with their start and end apart: 1, of which 1 were waited for; matrix products, arithmetic and copies ran while one was open for 0% of the time, Pallas kernels for 1%

profile of v10, /device:TPU:0, one launch (start us, length us, event | category | flops | bytes accessed | tf_op | source)
XLA Modules:
  0.0 19.5 jit_solution(14101060838456893941)
XLA Ops:
  0.6 1.9 %first.1 = bf16[32,16,128]{2,1,0:T(8,128)(2,1)S(1)} custom-call(bf16[256,2048]{1,0:T(8,128)(2,1)} %dosage.1, f32[1,2048]{1,0:T(1,128)} %bitcast.2, bf16[8,256]{1,0:T(8,128)(2,1)} %probes.3), custom_call_target="tpu_custom_call" | custom-call | tf_op jit(solution)/shard_map/first/pallas_call | solution.py:190
  2.5 14.9 %all_to_all.5.got = bf16[32,16,128]{2,1,0:T(8,128)(2,1)S(1)} all-to-all(bf16[32,16,128]{2,1,0:T(8,128)(2,1)S(1)} %first.1), channel_id=1, replica_groups=mesh['snp'=8,'probe'=4] {'probe','snp'}, dimensions={0} | all-to-all | bytes 262144 | tf_op jit(solution)/shard_map/all_to_all | solution.py:207
  17.5 0.0 copy-start
  17.5 0.2 collective-permute-start
  17.7 0.5 %copy-done = bf16[8,256]{1,0:T(8,128)(2,1)S(1)} copy-done((bf16[8,256]{1,0:T(8,128)(2,1)S(1)}, bf16[8,256]{1,0:T(8,128)(2,1)}, u32[]{:S(2)}) %copy-start) | copy-done | bytes 4120
  18.1 0.1 near.1
  18.3 0.5 %collective-permute-done.other = f32[56,128]{1,0:T(8,128)S(1)} collective-permute-done((f32[56,128]{1,0:T(8,128)S(1)}, f32[56,128]{1,0:T(8,128)S(1)}, u32[]{:S(2)}, u32[]{:S(2)}) %collective-permute-start) | collective-permute-done | bytes 28704 | tf_op jit(solution)/shard_map/ppermute | solution.py:220
  18.8 0.7 %last.1 = (f32[8,32]{1,0:T(8,128)}, f32[2,8]{1,0:T(2,128)}, f32[1,2]{1,0:T(1,128)}) custom-call(f32[56,128]{1,0:T(8,128)S(1)} %get-tuple-element.10.share, f32[56,128]{1,0:T(8,128)S(1)} %collective-permute-done.other, f32[8,128]{1,0:T(8,128)S(1)} %get-tuple-element.11.own, f32[8,32]{1,0:T(8,128)S(1)} %get-tuple-element.12.near_twice, ...), custom_call_target="tpu_custom_call" | custom-call | tf_op jit(solution)/shard_map/last/pallas_call | solution.py:232
  (1 shorter events, 0.0 us)
Async XLA Ops:
  17.5 0.7 %copy-start = (bf16[8,256]{1,0:T(8,128)(2,1)S(1)}, bf16[8,256]{1,0:T(8,128)(2,1)}, u32[]{:S(2)}) copy-start(bf16[8,256]{1,0:T(8,128)(2,1)} %probes.3) | copy-start | bytes 12292
  17.5 1.3 %collective-permute-start = (f32[56,128]{1,0:T(8,128)S(1)}, f32[56,128]{1,0:T(8,128)S(1)}, u32[]{:S(2)}, u32[]{:S(2)}) collective-permute-start(f32[56,128]{1,0:T(8,128)S(1)} %get-tuple-element.10.share), channel_id=1, source_target_pairs={{0,1},{1,0},{2,3},{3,2},{4,5},{5,4},{6,7},{7,6},{8,9},{9,8},{10,11... | collective-permute-start | bytes 86024 | tf_op jit(solution)/shard_map/ppermute | solution.py:220

commit v11 on v8

--- a/solution.py
+++ b/solution.py
@@ -37,7 +37,6 @@
                         (dosages - mean[:, at]) * scaling[:, at]
                     ).astype(jnp.bfloat16)
                     pltpu.matmul_push_rhs(standard[c, :, tile(k, q)], k, q)
-            for k in (0, 1):
                 for q in (0, 1):
                     pltpu.matmul_acc_lhs(raws[q][k], left, load_staged_rhs=k)
                     pltpu.matmul_push_rhs(standard[c, :, tile(k, q)], k, q, transpose=True)

time: 19.7 us -> 19.7 us (level)
  no operation moved by 1% of the time
where the time goes in v11:
time: 19.7 us; the launch traced here: 19.5 us
  blocking collectives  14.9 us (76%)
  Pallas kernels  2.65 us (13%)
  waiting for transfers between devices  1.09 us (6%)
  between operations  0.64 us (3%)
    all_to_all x1, blocking collectives, body(): got = lax.all_to_all(send, BOTH, 0, 0, tiled=True)  14.9 us
    pallas_call x1, Pallas kernels, body(): pl.pallas_call(functools.partial(first_kernel, snp_count=snp_count, probe...  1.89 us
    ppermute x1, waiting for transfers between devices, body(): lax.ppermute(share, 'probe', [(q, q ^ 1) for q in range(probe_count)])  1.09 us
    pallas_call x1, Pallas kernels, body(): pl.pallas_call(functools.partial(last_kernel, probe_count=probe_count), i...  0.73 us
  transfers between devices with their start and end apart: 1, of which 1 were waited for; matrix products, arithmetic and copies ran while one was open for 0% of the time, Pallas kernels for 0%

profile of v11, /device:TPU:0, one launch (start us, length us, event | category | flops | bytes accessed | tf_op | source)
XLA Modules:
  0.0 19.5 jit_solution(7182920642855155202)
XLA Ops:
  0.6 1.9 %first.1 = bf16[32,16,128]{2,1,0:T(8,128)(2,1)S(1)} custom-call(bf16[256,2048]{1,0:T(8,128)(2,1)} %dosage.1, f32[1,2048]{1,0:T(1,128)} %bitcast.2, bf16[8,256]{1,0:T(8,128)(2,1)} %probes.1), custom_call_target="tpu_custom_call" | custom-call | tf_op jit(solution)/shard_map/first/pallas_call | solution.py:183
  2.5 14.9 %all_to_all.5.got = bf16[32,16,128]{2,1,0:T(8,128)(2,1)S(1)} all-to-all(bf16[32,16,128]{2,1,0:T(8,128)(2,1)S(1)} %first.1), channel_id=1, replica_groups=mesh['snp'=8,'probe'=4] {'probe','snp'}, dimensions={0} | all-to-all | bytes 262144 | tf_op jit(solution)/shard_map/all_to_all | solution.py:200
  17.5 0.0 copy-start
  17.5 0.2 collective-permute-start
  17.7 1.1 %collective-permute-done.other = f32[56,128]{1,0:T(8,128)S(1)} collective-permute-done((f32[56,128]{1,0:T(8,128)S(1)}, f32[56,128]{1,0:T(8,128)S(1)}, u32[]{:S(2)}, u32[]{:S(2)}) %collective-permute-start) | collective-permute-done | bytes 28704 | tf_op jit(solution)/shard_map/ppermute | solution.py:213
  18.8 0.0 copy-done
  18.8 0.7 %last.1 = (f32[8,32]{1,0:T(8,128)}, f32[2,8]{1,0:T(2,128)}, f32[1,2]{1,0:T(1,128)}) custom-call(f32[56,128]{1,0:T(8,128)S(1)} %get-tuple-element.8.share, f32[56,128]{1,0:T(8,128)S(1)} %collective-permute-done.other, f32[8,128]{1,0:T(8,128)S(1)} %get-tuple-element.9.own, bf16[8,256]{1,0:T(8,128)(2,1)S(1)} %copy-done), custom_call_target="tpu_custom_call" | custom-call | tf_op jit(solution)/shard_map/last/pallas_call | solution.py:214
  (1 shorter events, 0.0 us)
Async XLA Ops:
  17.5 1.3 %copy-start = (bf16[8,256]{1,0:T(8,128)(2,1)S(1)}, bf16[8,256]{1,0:T(8,128)(2,1)}, u32[]{:S(2)}) copy-start(bf16[8,256]{1,0:T(8,128)(2,1)} %probes.1) | copy-start | bytes 12292
  17.5 1.3 %collective-permute-start = (f32[56,128]{1,0:T(8,128)S(1)}, f32[56,128]{1,0:T(8,128)S(1)}, u32[]{:S(2)}, u32[]{:S(2)}) collective-permute-start(f32[56,128]{1,0:T(8,128)S(1)} %get-tuple-element.8.share), channel_id=1, source_target_pairs={{0,1},{1,0},{2,3},{3,2},{4,5},{5,4},{6,7},{7,6},{8,9},{9,8},{10,11... | collective-permute-start | bytes 86024 | tf_op jit(solution)/shard_map/ppermute | solution.py:213
